TPU v7x, 256 devices: a whole 4x4x8 slice. The times are simulated.
256 devices in a mesh: seq: 128 (over y_hi, x, z, core), grp: 2 (over y_lo).
Axes of the slice: x: 4, y: 4 (y_hi: 2, y_lo: 2; y = y_hi * 2 + y_lo), z: 8, core: 2. Of those that a mesh axis runs over, the one named last changes fastest.
Arguments:
- prefill_queries: bfloat16 [8192, 4096], P('seq', 'grp'), may hold values from -6 to 6
- prefill_keys: bfloat16 [8192, 512], P('seq', 'grp'), may hold values from -6 to 6
- prefill_values: bfloat16 [8192, 512], P('seq', 'grp'), may hold values from -6 to 6
- block_mask: int32 [128, 128], replicated, may hold values 0 or 1
- bit_widths: int32 [4], P('grp'), may hold values from 3 to 8
- scale_exps: int32 [4], P('grp'), may hold values from 1 to 4
- decode_queries: bfloat16 [4, 256, 4096], P(None, 'seq', 'grp'), may hold values from -6 to 6
- new_keys: bfloat16 [4, 256, 512], P(None, 'seq', 'grp'), may hold values from -6 to 6
- new_values: bfloat16 [4, 256, 512], P(None, 'seq', 'grp'), may hold values from -6 to 6
- context_len: int32 [256], P('seq'), may hold values from 1 to 8192
Outputs:
- prefill_out: bfloat16 [8192, 4096], P('seq', 'grp')
- decode_out: bfloat16 [4, 256, 4096], P(None, 'seq', 'grp')
All inputs are finite; a program needn't handle non-finite values.
Results may differ from a plain program's by a relative error of at most 0.012.
Values may be sent and summed in bfloat16 or wider, within the bound.
A program may use at most 64 MiB of HBM per device.

v0:
```python
import math

import jax
import jax.numpy as jnp
from jax import lax
from jax.sharding import PartitionSpec as P

HEADS = 32
KV_HEADS = 4
HEAD = 128
STEPS = 4


very_low = -1e30
norm_eps = 1e-06


def sent_together(arrays, axis, dim, along):
    both = jnp.concatenate(arrays, axis=along)
    out, at, finished = (lax.all_gather(both, axis, axis=dim, tiled=True), 0, [])
    for a in arrays:
        finished.append(lax.slice_in_dim(out, at, at + a.shape[along], axis=along))
        at += a.shape[along]
    return tuple(finished)


def copy_for_each(shard, axis):
    copies = jnp.broadcast_to(shard, (lax.axis_size(axis), *shard.shape))
    return lax.all_to_all(copies, axis, split_axis=0, concat_axis=0, tiled=True)


def taken_together(shard, axis):
    return copy_for_each(shard, axis).sum(axis=0)


def together(arrays, axis):
    ends = [0]
    for a in arrays:
        ends.append(ends[-1] + a.size)
    running = taken_together(jnp.concatenate([a.ravel() for a in arrays]), axis)
    return tuple((running[b:e].reshape(a.shape) for a, b, e in zip(arrays, ends, ends[1:])))


def sign_table(order):
    positions = jnp.arange(order, dtype=jnp.int32)
    common_bits = positions[:, None] & positions[None, :]
    parity = jnp.zeros((order, order), jnp.int32)
    for bit_number in range(order.bit_length() - 1):
        parity = parity + (common_bits >> bit_number & 1)
    return (1 - 2 * (parity % 2)).astype(jnp.float32)


def level_terms(bit_widths, scale_exps):
    clip_level = 2.0 ** (bit_widths.astype(jnp.float32) - 1.0) - 1.0
    forward = 2.0 ** scale_exps.astype(jnp.float32) / math.sqrt(HEAD)
    backward = 2.0 ** (-scale_exps.astype(jnp.float32)) / math.sqrt(HEAD)
    return (clip_level, forward, backward)


def online_update(carried, scores, allowed, values, pattern):
    running_max, weight_sum, weighted = carried
    masked = jnp.where(allowed, scores, very_low)
    new_max = jnp.maximum(running_max, jnp.max(masked, axis=-1))
    factor = jnp.exp(running_max - new_max)
    weights = jnp.where(allowed, jnp.exp(masked - new_max[..., None]), 0.0)
    weight_sum = weight_sum * factor + jnp.sum(weights, axis=-1)
    weighted = weighted * factor[..., None] + jnp.einsum(
        pattern, weights.astype(jnp.bfloat16), values, preferred_element_type=jnp.float32
    )
    return (new_max, weight_sum, weighted)


def in_blocks(fold_fn, carried, arrays):
    count_rows = arrays[0].shape[0]
    block_rows = math.gcd(count_rows, 1024)
    number = count_rows // block_rows
    stacked = tuple((array.reshape((number, block_rows) + array.shape[1:]) for array in arrays))

    def advance(running, scan_item):
        position, pieces = scan_item
        return (fold_fn(running, pieces, position * block_rows), None)

    carried, _ = lax.scan(advance, carried, (jnp.arange(number, dtype=jnp.int32), stacked))
    return carried


def local(
    prefill_queries,
    prefill_keys,
    prefill_values,
    block_mask,
    bit_widths,
    scale_exps,
    decode_queries,
    new_keys,
    new_values,
    context_len,
):
    local_tokens = prefill_queries.shape[0]
    kv_local = bit_widths.shape[0]
    group_size = HEADS // KV_HEADS
    row_count = context_len.shape[0]
    full_width = HEADS * HEAD
    score_scale = 1.0 / math.sqrt(HEAD)
    seq_index = lax.axis_index("seq")
    sign_matrix = sign_table(HEAD).astype(jnp.bfloat16)
    clip_level, forward, backward = level_terms(bit_widths, scale_exps)
    queries = prefill_queries.reshape(local_tokens, kv_local, group_size, HEAD)
    query_pos = seq_index * local_tokens + jnp.arange(local_tokens, dtype=jnp.int32)
    mask_row = block_mask[seq_index]
    block_ids = jnp.arange(mask_row.shape[0], dtype=jnp.int32)

    def encode(rows):
        shaped = rows.reshape(rows.shape[0], kv_local, HEAD)
        rotated = jnp.dot(shaped, sign_matrix, preferred_element_type=jnp.float32)
        levels = jnp.floor(rotated * forward[:, None] + 0.5)
        limited = jnp.clip(levels, -clip_level[:, None], clip_level[:, None])
        return limited.astype(jnp.bfloat16).reshape(rows.shape[0], kv_local * HEAD)

    def restore(rows):
        shaped = rows.reshape(rows.shape[0], kv_local, HEAD)
        restored = jnp.dot(shaped, sign_matrix, preferred_element_type=jnp.float32)
        return (restored * backward[:, None]).astype(jnp.bfloat16)

    def attend(carried, pieces, offset):
        key_rows, value_rows = pieces
        count_rows = key_rows.shape[0]
        key_shaped = key_rows.reshape(count_rows, kv_local, HEAD)
        value_shaped = value_rows.reshape(count_rows, kv_local, HEAD)
        scores = (
            jnp.einsum("tkgd,skd->tkgs", queries, key_shaped, preferred_element_type=jnp.float32)
            * score_scale
        )
        key_pos = offset + jnp.arange(count_rows, dtype=jnp.int32)
        key_block = key_pos // local_tokens
        block_open = jnp.sum(
            jnp.where(key_block[:, None] == block_ids[None, :], mask_row[None, :], 0), axis=1
        )
        allowed = (key_pos[None, :] <= query_pos[:, None]) & (
            (key_block == seq_index) | (block_open == 1)
        )[None, :]
        return online_update(
            carried, scores, allowed[:, None, None, :], value_shaped, "tkgs,skd->tkgd"
        )

    def attend_keep(carried, pieces, offset):
        running, key_store, value_store = carried
        running = in_blocks(attend, running, pieces)
        key_store = encode(pieces[0])
        value_store = encode(pieces[1])
        return (running, key_store, value_store)

    start_shape = (local_tokens, kv_local, group_size)
    start_state = (
        jnp.full(start_shape, very_low, jnp.float32),
        jnp.zeros(start_shape, jnp.float32),
        jnp.zeros(start_shape + (HEAD,), jnp.float32),
    )
    empty_store = jnp.zeros((local_tokens * lax.axis_size("seq"), kv_local * HEAD), jnp.bfloat16)
    fold_fn, initial = (attend_keep, (start_state, empty_store, empty_store))
    folded = fold_fn(
        initial, sent_together((prefill_keys, prefill_values), "seq", 0, 1), jnp.int32(0)
    )
    dec_shaped = decode_queries.reshape(STEPS, row_count, kv_local, group_size, HEAD)

    def decode_step(carried, pieces, offset):
        key_rows, value_rows = pieces
        count_rows = key_rows.shape[0]
        key_plain = restore(key_rows)
        value_plain = restore(value_rows)
        scores = (
            jnp.einsum(
                "trkgd,pkd->trkgp", dec_shaped, key_plain, preferred_element_type=jnp.float32
            )
            * score_scale
        )
        key_pos = offset + jnp.arange(count_rows, dtype=jnp.int32)
        allowed = (key_pos[None, :] < context_len[:, None])[None, :, None, None, :]
        return online_update(carried, scores, allowed, value_plain, "trkgp,pkd->trkgd")

    dec_shape = (STEPS, row_count, kv_local, group_size)
    dec_state = (
        jnp.full(dec_shape, very_low, jnp.float32),
        jnp.zeros(dec_shape, jnp.float32),
        jnp.zeros(dec_shape + (HEAD,), jnp.float32),
    )
    prefill_state, key_store, value_store = folded
    dec_state = in_blocks(decode_step, dec_state, (key_store, value_store))
    own_keys = new_keys.reshape(STEPS, row_count, kv_local, HEAD)
    own_values = new_values.reshape(STEPS, row_count, kv_local, HEAD)
    own_scores = (
        jnp.einsum("trkgd,urkd->trkgu", dec_shaped, own_keys, preferred_element_type=jnp.float32)
        * score_scale
    )
    step_pos = jnp.arange(STEPS, dtype=jnp.int32)
    own_open = (step_pos[None, :] <= step_pos[:, None])[:, None, None, None, :]
    dec_state = online_update(dec_state, own_scores, own_open, own_values, "trkgu,urkd->trkgd")
    prefill_attn = (prefill_state[2] / prefill_state[1][..., None]).reshape(
        local_tokens, kv_local * group_size * HEAD
    )
    decode_attn = (dec_state[2] / dec_state[1][..., None]).reshape(
        STEPS, row_count, kv_local * group_size * HEAD
    )
    prefill_squares, decode_squares = together(
        (
            jnp.sum(prefill_attn * prefill_attn, axis=-1),
            jnp.sum(decode_attn * decode_attn, axis=-1),
        ),
        "grp",
    )
    prefill_out = (
        prefill_attn * lax.rsqrt(prefill_squares[:, None] / full_width + norm_eps)
    ).astype(jnp.bfloat16)
    decode_out = (
        decode_attn * lax.rsqrt(decode_squares[..., None] / full_width + norm_eps)
    ).astype(jnp.bfloat16)
    return (prefill_out, decode_out)


def solution(mesh):
    placed = (
        P("seq", "grp"),
        P("seq", "grp"),
        P("seq", "grp"),
        P(),
        P("grp"),
        P("grp"),
        P(None, "seq", "grp"),
        P(None, "seq", "grp"),
        P(None, "seq", "grp"),
        P("seq"),
    )
    return jax.shard_map(
        local,
        mesh=mesh,
        in_specs=placed,
        out_specs=(P("seq", "grp"), P(None, "seq", "grp")),
        check_vma=False,
    )
```

profile of v0, /device:TPU:1, one launch (start us, length us, event | category | flops | bytes accessed | tf_op | source)
XLA Modules:
  0.0 355.9 jit_solution(14918573249043709593)
XLA Ops:
  7.2 1.4 pad_maximum_fusion
  10.9 1.0 copy.168
  13.6 131.2 %all-gather.2.cloned.1.call-done = bf16[8192,512]{1,0:T(8,128)(2,1)} async-done(((bf16[64,512]{1,0:T(8,128)(2,1)}), bf16[8192,512]{1,0:T(8,128)(2,1)}) %all-gather.2.cloned.1.call-update) | async-done | bytes 8388624 | tf_op jit(solution)/shard_map/all_gather | solution.py:20
  144.8 5.7 %fusion.151 = (bf16[8192,256]{1,0:T(8,128)(2,1)}, bf16[8192,256]{1,0:T(8,128)(2,1)}) fusion(bf16[8192,512]{1,0:T(8,128)(2,1)} %all-gather.2.cloned.1.call-done), kind=kLoop, calls=%fused_computation.176 | loop fusion | bytes 16777216 | tf_op jit(solution)/shard_map/slice | solution.py:22
  150.5 6.4 %copy.164 = bf16[8192,256]{0,1:T(8,128)(2,1)} copy(bf16[8192,256]{1,0:T(8,128)(2,1)} %get-tuple-element.488) | data formatting | bytes 8388608
  156.9 7.2 %fusion.102 = bf16[8192,2,128]{2,0,1:T(8,128)(2,1)} fusion(bf16[8192,2,128]{0,2,1:T(8,128)(2,1)} %bitcast.167, f32[2]{0:T(128)S(1)} %get-tuple-element.490, bf16[2]{0:T(256)(128)(2,1)S(1)} %get-tuple-element.492, bf16[2]{0:T(256)(128)(2,1)S(1)} %get-tuple-element.491), kind=kOutput, calls=%fused_computation.106 | convolution fusion | flops 554237952 | bytes 8388624 | tf_op jit(solution)/shard_map/dot_general | solution.py:115
  164.1 6.3 %copy.130 = bf16[8192,2,128]{0,2,1:T(8,128)(2,1)} copy(bf16[8192,2,128]{2,0,1:T(8,128)(2,1)} %fusion.102) | data formatting | bytes 8388608 | tf_op jit(solution)/shard_map/convert_element_type | solution.py:118
  170.4 6.5 %copy.170 = bf16[32,8,8,1024]{3,2,1,0:T(8,128)(2,1)S(1)} copy(bf16[32,8,8,1024]{3,1,2,0:T(8,128)(2,1)} %bitcast.163) | data formatting | bytes 8388608
  176.9 4.3 %copy.133 = bf16[8,1024,256]{1,2,0:T(8,128)(2,1)} copy(bf16[8,1024,256]{1,0,2:T(8,128)(2,1)S(1)} %bitcast.164) | data formatting | bytes 8388608
  181.2 6.4 %copy.165 = bf16[8192,256]{0,1:T(8,128)(2,1)} copy(bf16[8192,256]{1,0:T(8,128)(2,1)} %get-tuple-element.487) | data formatting | bytes 8388608
  187.6 7.2 %fusion.101 = bf16[8192,2,128]{2,0,1:T(8,128)(2,1)} fusion(bf16[8192,2,128]{0,2,1:T(8,128)(2,1)} %bitcast.169, f32[2]{0:T(128)S(1)} %get-tuple-element.490, bf16[2]{0:T(256)(128)(2,1)S(1)} %get-tuple-element.492, bf16[2]{0:T(256)(128)(2,1)S(1)} %get-tuple-element.491), kind=kOutput, calls=%fused_computation.105 | convolution fusion | flops 554237952 | bytes 8388624 | tf_op jit(solution)/shard_map/dot_general | solution.py:115
  194.8 6.4 %copy.132 = bf16[8192,2,128]{0,2,1:T(8,128)(2,1)} copy(bf16[8192,2,128]{2,0,1:T(8,128)(2,1)} %fusion.101) | data formatting | bytes 8388608 | tf_op jit(solution)/shard_map/convert_element_type | solution.py:118
  201.1 6.5 %copy.171 = bf16[32,8,8,1024]{3,2,1,0:T(8,128)(2,1)S(1)} copy(bf16[32,8,8,1024]{3,1,2,0:T(8,128)(2,1)} %bitcast.165) | data formatting | bytes 8388608
  207.7 4.3 %copy.135 = bf16[8,1024,256]{1,2,0:T(8,128)(2,1)} copy(bf16[8,1024,256]{1,0,2:T(8,128)(2,1)S(1)} %bitcast.166) | data formatting | bytes 8388608
  212.0 35.6 %while.34 = (s32[]{:T(128)}, f32[4,2,2,8]{3,1,0,2:T(2,128)S(1)}, f32[4,2,2,8]{3,1,0,2:T(2,128)S(1)}, f32[4,2,2,8,128]{4,3,1,0,2:T(8,128)S(1)}, s32[8]{0:T(128)S(...) while((s32[]{:T(128)}, f32[4,2,2,8]{3,1,0,2:T(2,128)S(1)}, ...), condition=%wide.region_9.10_spmd.clone.clone, body=%wide.region_6.9_spmd.clone.clone.sunk | while | flops 204787328 | bytes 4907201 | solution.py:83
  213.3 1.3 constant_dynamic-slice_fusion.8
  214.5 0.9 fusion.194
  217.7 1.3 constant_dynamic-slice_fusion.8
  222.1 1.3 constant_dynamic-slice_fusion.8
  223.4 0.9 fusion.194
  226.5 1.3 constant_dynamic-slice_fusion.8
  231.0 1.3 constant_dynamic-slice_fusion.8
  232.2 0.9 fusion.194
  235.4 1.3 constant_dynamic-slice_fusion.8
  239.8 1.3 constant_dynamic-slice_fusion.8
  241.1 0.9 fusion.194
  244.2 1.3 constant_dynamic-slice_fusion.8
  248.2 6.1 %copy_bitcast_fusion = (bf16[8,1024,256]{1,2,0:T(8,128)(2,1)}, bf16[8,1024,256]{1,2,0:T(8,128)(2,1)}) fusion(bf16[32,8,8,1024]{3,2,1,0:T(8,128)(2,1)} %bitcast.170, bf16[32,8,8,1024]{3,2,1,0:T(8,128)(2,1)} %bitcast.168), kind=kLoop, calls=%fused_computation.107 | loop fusion | bytes 16777216
  254.3 86.3 %while.33 = (s32[]{:T(128)}, f32[64,2,8]{0,2,1:T(8,128)S(1)}, f32[64,2,8]{0,2,1:T(8,128)S(1)}, f32[64,2,8,128]{3,0,2,1:T(8,128)S(1)}, s32[8]{0:T(128)S(1)}, /*in...) while((s32[]{:T(128)}, f32[64,2,8]{0,2,1:T(8,128)S(1)}, ...), condition=%wide.region_4.5_spmd.clone, body=%wide.region_0.4_spmd.clone.sunk | while | flops 551459904 | bytes 34172120 | solution.py:83
  256.1 1.3 constant_dynamic-slice_fusion.7
  257.4 2.7 fusion.184
  260.1 3.6 %fusion.185 = f32[64,2,8]{0,2,1:T(8,128)S(1)} fusion(f32[2,1024,64,8]{1,2,3,0:T(8,128)} %get-tuple-element.635, f32[64,2,8]{0,2,1:T(8,128)S(1)} %select_maximum_fusion.2, pred[64,1024]{1,0:T(8,128)(4,1)S(1)} %compare_and_fusion.2), kind=kLoop, calls=%fused_computation.7.clone.1 | loop fusion | flops 5241856 | bytes 4268032 | tf_op jit(solution)/shard_map/while/body/eval_jaxpr/reduce_sum | solution.py:66
  263.7 1.3 fusion.187
  266.9 1.3 constant_dynamic-slice_fusion.7
  268.1 2.7 fusion.184
  270.9 3.6 %fusion.185 = f32[64,2,8]{0,2,1:T(8,128)S(1)} fusion(f32[2,1024,64,8]{1,2,3,0:T(8,128)} %get-tuple-element.635, f32[64,2,8]{0,2,1:T(8,128)S(1)} %select_maximum_fusion.2, pred[64,1024]{1,0:T(8,128)(4,1)S(1)} %compare_and_fusion.2), kind=kLoop, calls=%fused_computation.7.clone.1 | loop fusion | flops 5241856 | bytes 4268032 | tf_op jit(solution)/shard_map/while/body/eval_jaxpr/reduce_sum | solution.py:66
  274.5 1.3 fusion.187
  277.7 1.3 constant_dynamic-slice_fusion.7
  278.9 2.7 fusion.184
  281.7 3.6 %fusion.185 = f32[64,2,8]{0,2,1:T(8,128)S(1)} fusion(f32[2,1024,64,8]{1,2,3,0:T(8,128)} %get-tuple-element.635, f32[64,2,8]{0,2,1:T(8,128)S(1)} %select_maximum_fusion.2, pred[64,1024]{1,0:T(8,128)(4,1)S(1)} %compare_and_fusion.2), kind=kLoop, calls=%fused_computation.7.clone.1 | loop fusion | flops 5241856 | bytes 4268032 | tf_op jit(solution)/shard_map/while/body/eval_jaxpr/reduce_sum | solution.py:66
  285.3 1.3 fusion.187
  288.4 1.3 constant_dynamic-slice_fusion.7
  289.7 2.7 fusion.184
  292.5 3.6 %fusion.185 = f32[64,2,8]{0,2,1:T(8,128)S(1)} fusion(f32[2,1024,64,8]{1,2,3,0:T(8,128)} %get-tuple-element.635, f32[64,2,8]{0,2,1:T(8,128)S(1)} %select_maximum_fusion.2, pred[64,1024]{1,0:T(8,128)(4,1)S(1)} %compare_and_fusion.2), kind=kLoop, calls=%fused_computation.7.clone.1 | loop fusion | flops 5241856 | bytes 4268032 | tf_op jit(solution)/shard_map/while/body/eval_jaxpr/reduce_sum | solution.py:66
  296.1 1.3 fusion.187
  299.2 1.3 constant_dynamic-slice_fusion.7
  300.5 2.7 fusion.184
  303.3 3.6 %fusion.185 = f32[64,2,8]{0,2,1:T(8,128)S(1)} fusion(f32[2,1024,64,8]{1,2,3,0:T(8,128)} %get-tuple-element.635, f32[64,2,8]{0,2,1:T(8,128)S(1)} %select_maximum_fusion.2, pred[64,1024]{1,0:T(8,128)(4,1)S(1)} %compare_and_fusion.2), kind=kLoop, calls=%fused_computation.7.clone.1 | loop fusion | flops 5241856 | bytes 4268032 | tf_op jit(solution)/shard_map/while/body/eval_jaxpr/reduce_sum | solution.py:66
  306.9 1.3 fusion.187
  310.0 1.3 constant_dynamic-slice_fusion.7
  311.3 2.7 fusion.184
  314.0 3.6 %fusion.185 = f32[64,2,8]{0,2,1:T(8,128)S(1)} fusion(f32[2,1024,64,8]{1,2,3,0:T(8,128)} %get-tuple-element.635, f32[64,2,8]{0,2,1:T(8,128)S(1)} %select_maximum_fusion.2, pred[64,1024]{1,0:T(8,128)(4,1)S(1)} %compare_and_fusion.2), kind=kLoop, calls=%fused_computation.7.clone.1 | loop fusion | flops 5241856 | bytes 4268032 | tf_op jit(solution)/shard_map/while/body/eval_jaxpr/reduce_sum | solution.py:66
  317.7 1.3 fusion.187
  320.8 1.3 constant_dynamic-slice_fusion.7
  322.1 2.7 fusion.184
  324.8 3.6 %fusion.185 = f32[64,2,8]{0,2,1:T(8,128)S(1)} fusion(f32[2,1024,64,8]{1,2,3,0:T(8,128)} %get-tuple-element.635, f32[64,2,8]{0,2,1:T(8,128)S(1)} %select_maximum_fusion.2, pred[64,1024]{1,0:T(8,128)(4,1)S(1)} %compare_and_fusion.2), kind=kLoop, calls=%fused_computation.7.clone.1 | loop fusion | flops 5241856 | bytes 4268032 | tf_op jit(solution)/shard_map/while/body/eval_jaxpr/reduce_sum | solution.py:66
  328.5 1.3 fusion.187
  331.6 1.3 constant_dynamic-slice_fusion.7
  332.9 2.7 fusion.184
  335.6 3.6 %fusion.185 = f32[64,2,8]{0,2,1:T(8,128)S(1)} fusion(f32[2,1024,64,8]{1,2,3,0:T(8,128)} %get-tuple-element.635, f32[64,2,8]{0,2,1:T(8,128)S(1)} %select_maximum_fusion.2, pred[64,1024]{1,0:T(8,128)(4,1)S(1)} %compare_and_fusion.2), kind=kLoop, calls=%fused_computation.7.clone.1 | loop fusion | flops 5241856 | bytes 4268032 | tf_op jit(solution)/shard_map/while/body/eval_jaxpr/reduce_sum | solution.py:66
  339.3 1.3 fusion.187
  341.6 3.2 all-to-all-start
  345.1 2.2 all-to-all-done
  348.2 0.9 fusion.107
  (199 shorter events, 32.0 us)
Async XLA Ops:
  7.2 4.8 %copy-start = (s32[128,128]{1,0:T(8,128)S(1)}, s32[128,128]{1,0:T(8,128)}, u32[]{:S(2)}) copy-start(s32[128,128]{1,0:T(8,128)} %param.17) | copy-start | bytes 196612
  7.2 137.6 %all-gather.2.cloned.1.call-start = ((), (), s32[]{:S(2)}) async-start(), calls=%async_computation.1 | async-start | bytes 8454144 | tf_op jit(solution)/shard_map/all_gather | solution.py:20
  207.6 4.3 %copy-start.3 = (s32[2]{0:T(128)S(1)}, s32[2]{0:T(128)}, u32[]{:S(2)}) copy-start(s32[2]{0:T(128)} %param.23) | copy-start | bytes 28
  260.1 3.6 %copy-start.2 = (f32[2,1024,64,8]{1,2,3,0:T(8,128)S(1)}, f32[2,1024,64,8]{1,2,3,0:T(8,128)}, u32[]{:S(2)}) copy-start(f32[2,1024,64,8]{1,2,3,0:T(8,128)} %get-tuple-element.635) | copy-start | bytes 12582916 | tf_op jit(solution)/shard_map/while
  270.9 3.6 %copy-start.2 = (f32[2,1024,64,8]{1,2,3,0:T(8,128)S(1)}, f32[2,1024,64,8]{1,2,3,0:T(8,128)}, u32[]{:S(2)}) copy-start(f32[2,1024,64,8]{1,2,3,0:T(8,128)} %get-tuple-element.635) | copy-start | bytes 12582916 | tf_op jit(solution)/shard_map/while
  281.7 3.6 %copy-start.2 = (f32[2,1024,64,8]{1,2,3,0:T(8,128)S(1)}, f32[2,1024,64,8]{1,2,3,0:T(8,128)}, u32[]{:S(2)}) copy-start(f32[2,1024,64,8]{1,2,3,0:T(8,128)} %get-tuple-element.635) | copy-start | bytes 12582916 | tf_op jit(solution)/shard_map/while
  292.5 3.6 %copy-start.2 = (f32[2,1024,64,8]{1,2,3,0:T(8,128)S(1)}, f32[2,1024,64,8]{1,2,3,0:T(8,128)}, u32[]{:S(2)}) copy-start(f32[2,1024,64,8]{1,2,3,0:T(8,128)} %get-tuple-element.635) | copy-start | bytes 12582916 | tf_op jit(solution)/shard_map/while
  303.2 3.6 %copy-start.2 = (f32[2,1024,64,8]{1,2,3,0:T(8,128)S(1)}, f32[2,1024,64,8]{1,2,3,0:T(8,128)}, u32[]{:S(2)}) copy-start(f32[2,1024,64,8]{1,2,3,0:T(8,128)} %get-tuple-element.635) | copy-start | bytes 12582916 | tf_op jit(solution)/shard_map/while
  314.0 3.6 %copy-start.2 = (f32[2,1024,64,8]{1,2,3,0:T(8,128)S(1)}, f32[2,1024,64,8]{1,2,3,0:T(8,128)}, u32[]{:S(2)}) copy-start(f32[2,1024,64,8]{1,2,3,0:T(8,128)} %get-tuple-element.635) | copy-start | bytes 12582916 | tf_op jit(solution)/shard_map/while
  324.8 3.6 %copy-start.2 = (f32[2,1024,64,8]{1,2,3,0:T(8,128)S(1)}, f32[2,1024,64,8]{1,2,3,0:T(8,128)}, u32[]{:S(2)}) copy-start(f32[2,1024,64,8]{1,2,3,0:T(8,128)} %get-tuple-element.635) | copy-start | bytes 12582916 | tf_op jit(solution)/shard_map/while
  335.6 3.6 %copy-start.2 = (f32[2,1024,64,8]{1,2,3,0:T(8,128)S(1)}, f32[2,1024,64,8]{1,2,3,0:T(8,128)}, u32[]{:S(2)}) copy-start(f32[2,1024,64,8]{1,2,3,0:T(8,128)} %get-tuple-element.635) | copy-start | bytes 12582916 | tf_op jit(solution)/shard_map/while
  340.6 8.5 %copy-start.1 = (s32[128,128]{1,0:T(8,128)S(1)}, s32[128,128]{1,0:T(8,128)}, u32[]{:S(2)}) copy-start(s32[128,128]{1,0:T(8,128)} %param.17) | copy-start | bytes 196612
  341.6 5.7 %all-to-all-start = ((f32[2,1,72]{2,1,0:T(1,128)}), f32[2,1,72]{2,1,0:T(1,128)S(1)}, u32[]{:S(2)}, u32[]{:S(2)}) async-start(f32[2,1,72]{2,1,0:T(1,128)} %broadcast_in_dim.154), calls=%async_computation | async-start | bytes 2048 | tf_op jit(solution)/shard_map/all_to_all | solution.py:29
Sparse Core Ops, SparseCore 0:
  12.2 132.6 all-gather.1
where the time goes:
time: 357 us; the launch traced here: 356 us
  waiting for transfers between devices  133 us (37%)
  local copies, waits for them, and re-layouts  93.1 us (26%)
  matrix products  59.4 us (17%)
  other arithmetic  40.9 us (11%)
  between operations  14.2 us (4%)
  loops' own time  11.7 us (3%)
    all_gather x1, waiting for transfers between devices, sent_together(): lax.all_gather(both, axis, axis=dim, tiled=True)  131 us
    unnamed x16, local copies, waits for them, and re-layouts  41.5 us
    reduce_sum x17, other arithmetic, online_update(): weight_sum = weight_sum * factor + jnp.sum(weights, axis=-1)  31 us
    dynamic_slice x32, local copies, waits for them, and re-layouts, in_blocks(): lax.scan(advance, carried, (jnp.arange(number, dtype=jnp.int32), stacked))  29.7 us
    dot_general x8, matrix products, attend(): jnp.einsum('tkgd,skd->tkgs', queries, key_shaped, preferred_element_type=...  21.9 us
    dot_general x17, matrix products, online_update(): jnp.einsum(pattern, weights.astype(jnp.bfloat16), values, preferred_eleme...  16.1 us
    dot_general x2, matrix products, encode(): rotated = jnp.dot(shaped, sign_matrix, preferred_element_type=jnp.float32)  14.3 us
    convert_element_type x2, local copies, waits for them, and re-layouts, encode(): return limited.astype(jnp.bfloat16).reshape(rows.shape[0], kv_local * HEAD)  12.7 us
  transfers between devices with their start and end apart: 2, of which 2 were waited for; matrix products, arithmetic and copies ran while one was open for 1% of the time, Pallas kernels for 0%

commit v1 on v0

v1 whole, which is shorter than its diff:
```python
import math

import jax
import jax.numpy as jnp
import numpy as np
from jax import lax
from jax.experimental import pallas as pl
from jax.experimental.pallas import tpu as pltpu
from jax.sharding import PartitionSpec as P

HEADS = 32
KV = 2
GROUP = 8
HEAD = 128
STEPS = 4
TOK = 64
ROWS = 2
XS, ZS = 4, 8
HALF = TOK // 2
UNIT = 2 * HALF
TILE = 512
VERY_LOW = -1e30
EPS = 1e-6
WIDE = HEADS * HEAD
SCORE = math.log2(math.e) / math.sqrt(HEAD)

BF = jnp.bfloat16
F32 = jnp.float32
MESH = pl.DeviceIdType.MESH

OFFSETS = [(dx, dz) for dx in (0, -1, 1, 2) for dz in (0, -1, 1, -2, 2, -3, 3, 4)]
WAVES = [[o for o in OFFSETS if abs(o[0]) + abs(o[1]) == d] for d in range(7)]
SLOT = {}
START = []
for wave in WAVES:
    START.append(len(SLOT) * UNIT)
    for path in (0, 1):
        for off in wave:
            SLOT[(path, *off)] = len(SLOT)
START.append(len(SLOT) * UNIT)
OWN = START[-1]
NTILE = OWN // TILE
FIRST = [max(0, (START[d] // TILE)) for d in range(7)]
TABLE = np.array(
    [path * 64 + (dx % XS) * 8 + dz % ZS for (path, dx, dz) in SLOT], np.int32
)


def x_moves(dx):
    return {
        0: [("x", 1, -1, None), ("x", -1, 1, None)],
        -1: [("x", 1, 2, 0)],
        1: [("x", -1, 2, 1)],
        2: [],
    }[dx]


def z_moves(dz):
    if dz == 0:
        return [("z", 1, -1, None), ("z", -1, 1, None)]
    if dz == 4:
        return []
    way = 1 if dz < 0 else -1
    if abs(dz) == 3:
        return [("z", way, 4, 0 if dz < 0 else 1)]
    return [("z", way, dz - way, None)]


def moves(path, dx, dz):
    out = []
    if path == 0 or dx == 0:
        out += [(a, w, SLOT[(path, dx, n)], h) for a, w, n, h in z_moves(dz)]
    if path == 1 or dz == 0:
        out += [(a, w, SLOT[(path, n, dz)], h) for a, w, n, h in x_moves(dx)]
    return out


def dot(a, b):
    return jnp.dot(a, b, preferred_element_type=F32)


def choose(n, first, values):
    out = jnp.float32(values[0])
    for i, v in enumerate(values[1:]):
        out = jnp.where(n == first + 1 + i, jnp.float32(v), out)
    return out


def kernel(
    table,
    widths,
    exps,
    ctx,
    q_ref,
    k_hbm,
    v_hbm,
    k_own,
    v_own,
    mask_ref,
    dq_ref,
    nk_ref,
    nv_ref,
    out_ref,
    dout_ref,
    kv,
    qx,
    qd,
    h2,
    oh,
    pos,
    m_p,
    l_p,
    o_p,
    m_d,
    l_d,
    o_d,
    m_0,
    o_0,
    dq_s,
    nk_s,
    nv_s,
    attn,
    dattn,
    sq_mine,
    sq_theirs,
    load_sem,
    y_send,
    y_recv,
    send_sem,
    recv_sem,
    sib_send,
    sib_recv,
    g_send,
    g_recv,
):
    s = lax.axis_index("seq")
    grp = lax.axis_index("grp")
    core = s % 2
    z = (s // 2) % ZS
    x = (s // (2 * ZS)) % XS
    yh = s // (2 * ZS * XS)

    def at(yh_, x_, z_, core_):
        return ((yh_ * XS + x_) * ZS + z_) * 2 + core_

    peers = {
        ("x", 1): at(yh, (x + 1) % XS, z, core),
        ("x", -1): at(yh, (x + XS - 1) % XS, z, core),
        ("z", 1): at(yh, x, (z + 1) % ZS, core),
        ("z", -1): at(yh, x, (z + ZS - 1) % ZS, core),
    }
    across = at(1 - yh, x, z, core)
    sibling = at(yh, x, z, 1 - core)

    loads = []
    for path in (0, 1):
        for part, src in enumerate((k_hbm, v_hbm)):
            loads.append(
                pltpu.make_async_copy(
                    src.at[pl.ds(path * HALF, HALF), :],
                    kv.at[pl.ds(path * UNIT + yh * HALF, HALF), pl.ds(part * 256, 256)],
                    load_sem.at[path * 2 + part],
                )
            )
    for c in loads:
        c.start()

    barrier = pltpu.get_barrier_semaphore()
    for dev in (*peers.values(), across, sibling):
        pl.semaphore_signal(barrier, inc=1, device_id=(dev, grp), device_id_type=MESH)
    pl.semaphore_signal(barrier, inc=1, device_id=(s, 1 - grp), device_id_type=MESH)
    for c in loads:
        c.wait()
    pl.semaphore_wait(barrier, 7)

    def remote(src_row, dst_row, count, ssem, rsem, dev):
        return pltpu.make_async_remote_copy(
            src_ref=kv.at[pl.ds(src_row, count), :],
            dst_ref=kv.at[pl.ds(dst_row, count), :],
            send_sem=ssem,
            recv_sem=rsem,
            device_id=(dev, grp),
            device_id_type=MESH,
        )

    ycopies = []
    for path in (0, 1):
        row = path * UNIT + yh * HALF
        ycopies.append(remote(row, row, HALF, y_send.at[path], y_recv.at[path], across))
    for c in ycopies:
        c.start()

    i0 = lax.broadcasted_iota(jnp.int32, (256, 256), 0)
    i1 = lax.broadcasted_iota(jnp.int32, (256, 256), 1)
    both = (i0 & i1) & 127
    parity = jnp.zeros((256, 256), jnp.int32)
    for b in range(7):
        parity = parity + ((both >> b) & 1)
    sign = (1 - 2 * (parity % 2)).astype(F32)
    h2[...] = jnp.where((i0 // 128) == (i1 // 128), sign, 0.0).astype(BF)

    lane = lax.broadcasted_iota(jnp.int32, (1, 128), 1)
    first_head = lane < 64
    level = [choose(widths[i], 3, [3.0, 7.0, 15.0, 31.0, 63.0, 127.0]) for i in range(KV)]
    power = [choose(exps[i], 1, [2.0, 4.0, 8.0, 16.0]) for i in range(KV)]
    inverse = [choose(exps[i], 1, [0.5, 0.25, 0.125, 0.0625]) for i in range(KV)]
    forward = [p / math.sqrt(HEAD) for p in power]
    backward = [p / math.sqrt(HEAD) for p in inverse]
    limits = jnp.where(lane % 2 == 0, ctx[0], ctx[1])

    row = mask_ref[pl.ds(s, 1), :]
    closed = jnp.where((row == 1) & (lane < s), 0.0, VERY_LOW).astype(F32)
    tri = lax.broadcasted_iota(jnp.int32, (TOK, 512), 0) <= (
        lax.broadcasted_iota(jnp.int32, (TOK, 512), 1) % TOK
    )
    for kh in range(KV):
        for g in range(GROUP):
            h = kh * GROUP + g
            piece = q_ref[:, h * HEAD : (h + 1) * HEAD].astype(F32)
            cols = slice(g * TOK, (g + 1) * TOK)
            whole = jnp.concatenate([piece, jnp.broadcast_to(closed, (TOK, 128))], axis=1)
            if g % 2 == 0:
                held = whole
            else:
                two = jnp.concatenate([held, whole], axis=0)
                qx[kh, :, (g - 1) * TOK : (g + 1) * TOK] = two.T.astype(BF)
        sc = dot(k_own[:, kh * HEAD : (kh + 1) * HEAD], qx[kh, 0:128, :])
        sc = jnp.where(tri, sc, VERY_LOW)
        top = jnp.max(sc, axis=0, keepdims=True)
        w = jnp.exp2((sc - top) * SCORE)
        m_p[kh] = top
        l_p[kh] = jnp.sum(w, axis=0, keepdims=True)
        vt = v_own[:, kh * HEAD : (kh + 1) * HEAD].astype(F32).T.astype(BF)
        o_p[kh] = dot(vt, w.astype(BF))

    for h in range(KV * GROUP):
        for t in range(STEPS):
            dq_s[h * 8 + t * ROWS : h * 8 + (t + 1) * ROWS, :] = dq_ref[
                t, :, h * HEAD : (h + 1) * HEAD
            ].astype(F32)
    nk_s[...] = jnp.zeros_like(nk_s)
    nv_s[...] = jnp.zeros_like(nv_s)
    for t in range(STEPS):
        nk_s[t * ROWS : (t + 1) * ROWS, :] = nk_ref[t].astype(F32)
        nv_s[t * ROWS : (t + 1) * ROWS, :] = nv_ref[t].astype(F32)
    dq = dq_s[...]
    turned = dot(dq.astype(BF), h2[0:128, 0:128])
    which = lax.broadcasted_iota(jnp.int32, (128, 1), 0) < 64
    turned = (turned * jnp.where(which, backward[0], backward[1])).T
    high = turned.astype(BF).astype(F32)
    low = turned - high
    zero = jnp.zeros((128, 128), F32)
    for part, a in enumerate((high, low)):
        cols = slice(part * 128, (part + 1) * 128)
        qd[0:128, cols] = jnp.where(first_head, a, zero).astype(BF)
        qd[128:256, cols] = jnp.where(first_head, zero, a).astype(BF)
    dqt = dq.T
    upper = jnp.where(first_head, dqt, zero).astype(BF)
    lower = jnp.where(first_head, zero, dqt).astype(BF)
    nk = nk_s[...].astype(BF)
    sc = dot(nk[:, 0:128], upper) + dot(nk[:, 128:256], lower)
    key_i = lax.broadcasted_iota(jnp.int32, (128, 128), 0)
    qry_i = lax.broadcasted_iota(jnp.int32, (128, 128), 1) % (STEPS * ROWS)
    seen = (
        (key_i < STEPS * ROWS)
        & (key_i % ROWS == qry_i % ROWS)
        & (key_i // ROWS <= qry_i // ROWS)
    )
    sc = jnp.where(seen, sc, VERY_LOW)
    top = jnp.max(sc, axis=0, keepdims=True)
    w = jnp.where(seen, jnp.exp2((sc - top) * SCORE), 0.0)
    m_d[...] = top
    m_0[...] = top
    l_d[...] = jnp.sum(w, axis=0, keepdims=True)
    nvt = nv_s[...].T.astype(BF)
    wide = dot(nvt, w.astype(BF))
    o_0[...] = jnp.where(first_head, wide[0:128], wide[128:256])
    o_d[...] = jnp.zeros_like(o_d)

    def forwards(d):
        for path in (0, 1):
            for dx, dz in WAVES[d]:
                here = SLOT[(path, dx, dz)] * UNIT
                for axis, way, there, half in moves(path, dx, dz):
                    shift, count = (0, UNIT) if half is None else (half * HALF, HALF)
                    remote(
                        here + shift,
                        there * UNIT + shift,
                        count,
                        send_sem.at[d + 1],
                        recv_sem.at[d + 1],
                        peers[(axis, way)],
                    ).start()

    def wave_copy(d):
        return remote(
            START[d], START[d], START[d + 1] - START[d], send_sem.at[d], recv_sem.at[d], sibling
        )

    def to_sibling(d):
        return remote(
            START[d],
            OWN + START[d],
            START[d + 1] - START[d],
            sib_send.at[d],
            sib_recv.at[d],
            sibling,
        )

    for c in ycopies:
        c.wait_recv()
    forwards(0)
    to_sibling(0).start()

    def step(i, carry):
        for d in range(1, 7):
            at_step = 2 * max(FIRST[d], 0) if d > 1 else 0
            if d in (2,):
                at_step = 2 * 1

            @pl.when(i == at_step)
            def _():
                wave_copy(d).wait_recv()
                if d < 6:
                    forwards(d)
                to_sibling(d).start()

            @pl.when(i == at_step + 1)
            def _():
                if d == 1:
                    to_sibling(0).wait_recv()
                to_sibling(d).wait_recv()

        e = i % 2
        tile = i // 2
        first = pl.multiple_of(e * OWN + tile * TILE, TILE)
        rows_in = lax.broadcasted_iota(jnp.int32, (HALF, 128), 0)
        lanes_in = lax.broadcasted_iota(jnp.int32, (HALF, 128), 1)
        for u in range(TILE // UNIT):
            code = table[tile * (TILE // UNIT) + u]
            sx = (x + (code % 64) // 8) % XS
            sz = (z + code % 8) % ZS
            for y in (0, 1):
                block = at(y, sx, sz, (core + e) % 2)
                here = slice(u * UNIT + y * HALF, u * UNIT + (y + 1) * HALF)
                oh[here, :] = jnp.where(lanes_in == block, 1.0, 0.0).astype(BF)
                pos[here, :] = rows_in + (block * TOK + (code // 64) * HALF)

        keys = kv[pl.ds(first, TILE), 0:256]
        vals_t = kv[pl.ds(first, TILE), 256:512].T
        blocks = oh[...]
        for kh in range(KV):
            ext = jnp.concatenate([keys[:, kh * HEAD : (kh + 1) * HEAD], blocks], axis=1)
            sc = dot(ext, qx[kh])
            old = m_p[kh]
            top = jnp.maximum(old, jnp.max(sc, axis=0, keepdims=True))
            w = jnp.exp2(sc * SCORE - top * SCORE)
            fade = jnp.exp2((old - top) * SCORE)
            m_p[kh] = top
            l_p[kh] = l_p[kh] * fade + jnp.sum(w, axis=0, keepdims=True)
            o_p[kh] = o_p[kh] * fade + dot(vals_t[kh * HEAD : (kh + 1) * HEAD, :], w.astype(BF))

        rot = dot(keys, h2[...])
        coded = jnp.concatenate(
            [
                jnp.clip(
                    jnp.floor(rot[:, j * HEAD : (j + 1) * HEAD] * forward[j] + 0.5),
                    -level[j],
                    level[j],
                ).astype(BF)
                for j in range(KV)
            ],
            axis=1,
        )
        two = dot(coded, qd[...])
        sc = jnp.where(pos[...] < limits, two[:, 0:128] + two[:, 128:256], VERY_LOW)
        old = m_d[...]
        top = jnp.maximum(old, jnp.max(sc, axis=0, keepdims=True))
        w = jnp.exp2(sc * SCORE - top * SCORE)
        fade = jnp.exp2((old - top) * SCORE)
        m_d[...] = top
        l_d[...] = l_d[...] * fade + jnp.sum(w, axis=0, keepdims=True)
        rot = dot(h2[...], vals_t)
        coded = jnp.concatenate(
            [
                jnp.clip(
                    jnp.floor(rot[j * HEAD : (j + 1) * HEAD, :] * forward[j] + 0.5),
                    -level[j],
                    level[j],
                ).astype(BF)
                for j in range(KV)
            ],
            axis=0,
        )
        o_d[...] = o_d[...] * fade + dot(coded, w.astype(BF))
        return carry

    lax.fori_loop(0, 2 * NTILE, step, 0)

    turned = jnp.where(first_head, o_d[0:128, :], o_d[128:256, :])
    high = turned.astype(BF)
    low = (turned - high.astype(F32)).astype(BF)
    sign = h2[0:128, 0:128]
    plain = (dot(sign, high) + dot(sign, low)) * jnp.where(first_head, backward[0], backward[1])
    plain = plain + o_0[...] * jnp.exp2((m_0[...] - m_d[...]) * SCORE)
    dattn[...] = (plain / l_d[...]).T
    total = jnp.zeros((8, 128), F32)
    for h in range(KV * GROUP):
        a = dattn[h * 8 : (h + 1) * 8, :]
        total = total + a * a
    sq_mine[TOK : TOK + 8, :] = jnp.broadcast_to(jnp.sum(total, axis=1, keepdims=True), (8, 128))

    total = jnp.zeros((TOK, 128), F32)
    for kh in range(KV):
        done = (o_p[kh] / l_p[kh]).T
        attn[kh] = done
        for g in range(GROUP):
            a = done[g * TOK : (g + 1) * TOK, :]
            total = total + a * a
    sq_mine[0:TOK, :] = jnp.broadcast_to(jnp.sum(total, axis=1, keepdims=True), (TOK, 128))
    swap = pltpu.make_async_remote_copy(
        src_ref=sq_mine,
        dst_ref=sq_theirs,
        send_sem=g_send,
        recv_sem=g_recv,
        device_id=(s, 1 - grp),
        device_id_type=MESH,
    )
    swap.start()

    for c in ycopies:
        c.wait_send()
    for d in range(7):
        if d > 0:
            wave_copy(d).wait_send()
        to_sibling(d).wait_send()
    swap.wait()
    norm = lax.rsqrt((sq_mine[...] + sq_theirs[...]) / WIDE + EPS)
    for kh in range(KV):
        for g in range(GROUP):
            h = kh * GROUP + g
            out_ref[:, h * HEAD : (h + 1) * HEAD] = (
                attn[kh, g * TOK : (g + 1) * TOK, :] * norm[0:TOK]
            ).astype(BF)
            a = (dattn[h * 8 : (h + 1) * 8, :] * norm[TOK : TOK + 8]).astype(BF)
            for t in range(STEPS):
                dout_ref[t, :, h * HEAD : (h + 1) * HEAD] = a[t * ROWS : (t + 1) * ROWS, :]


def local(q, k, v, mask, widths, exps, dq, nk, nv, ctx):
    vmem = pl.BlockSpec(memory_space=pltpu.VMEM)
    smem = pl.BlockSpec(memory_space=pltpu.SMEM)
    anyw = pl.BlockSpec(memory_space=pl.ANY)
    dma = pltpu.SemaphoreType.DMA
    return pl.pallas_call(
        kernel,
        out_shape=(
            jax.ShapeDtypeStruct(q.shape, BF),
            jax.ShapeDtypeStruct(dq.shape, BF),
        ),
        in_specs=[smem] * 4 + [vmem, anyw, anyw] + [vmem] * 6,
        out_specs=(vmem, vmem),
        scratch_shapes=[
            pltpu.VMEM((2 * OWN, 512), BF),
            pltpu.VMEM((KV, 256, 512), BF),
            pltpu.VMEM((256, 256), BF),
            pltpu.VMEM((256, 256), BF),
            pltpu.VMEM((TILE, 128), BF),
            pltpu.VMEM((TILE, 128), jnp.int32),
            pltpu.VMEM((KV, 1, 512), F32),
            pltpu.VMEM((KV, 1, 512), F32),
            pltpu.VMEM((KV, 128, 512), F32),
            pltpu.VMEM((1, 128), F32),
            pltpu.VMEM((1, 128), F32),
            pltpu.VMEM((256, 128), F32),
            pltpu.VMEM((1, 128), F32),
            pltpu.VMEM((128, 128), F32),
            pltpu.VMEM((128, 128), F32),
            pltpu.VMEM((128, 256), F32),
            pltpu.VMEM((128, 256), F32),
            pltpu.VMEM((KV, 512, 128), F32),
            pltpu.VMEM((128, 128), F32),
            pltpu.VMEM((TOK + 8, 128), F32),
            pltpu.VMEM((TOK + 8, 128), F32),
            dma((4,)),
            dma((2,)),
            dma((2,)),
            dma((7,)),
            dma((7,)),
            dma((7,)),
            dma((7,)),
            dma,
            dma,
        ],
        compiler_params=pltpu.CompilerParams(
            collective_id=0, has_side_effects=True, vmem_limit_bytes=48 * 1024 * 1024
        ),
    )(jnp.asarray(TABLE), widths, exps, ctx, q, k, v, k, v, mask, dq, nk, nv)


def solution(mesh):
    placed = (
        P("seq", "grp"),
        P("seq", "grp"),
        P("seq", "grp"),
        P(),
        P("grp"),
        P("grp"),
        P(None, "seq", "grp"),
        P(None, "seq", "grp"),
        P(None, "seq", "grp"),
        P("seq"),
    )
    return jax.shard_map(
        local,
        mesh=mesh,
        in_specs=placed,
        out_specs=(P("seq", "grp"), P(None, "seq", "grp")),
        check_vma=False,
    )
```

time: 357 us -> 66.3 us (0.19)
  waiting for transfers between devices: 133 us -> 0 us
  local copies, waits for them, and re-layouts: 93.1 us -> 9.37 us
  matrix products: 59.4 us -> 0 us
  Pallas kernels: 0 us -> 55.8 us
  other arithmetic: 40.9 us -> 0 us
  between operations: 14.2 us -> 0.66 us
  loops' own time: 11.7 us -> 0 us
    all_gather x1 -> x0, waiting for transfers between devices: 131 us -> none  [sent_together(): lax.all_gather(both, axis, axis=dim, tiled=True)]
    dot_general x36 -> x0, matrix products: 59.4 us -> none  [the longest x8 21.9 us: attend(): jnp.einsum('tkgd,skd->tkgs', queries, key_shaped, preferred_element_type=...]
    pallas_call x0 -> x1, Pallas kernels: none -> 55.8 us  [local(): pl.pallas_call(kernel, out_shape=(jax.ShapeDtypeStruct(q.shape, BF), jax....]
    reduce_sum x27 -> x0, other arithmetic: 34.2 us -> none  [the longest x17 31 us: online_update(): weight_sum = weight_sum * factor + jnp.sum(weights, axis=-1)]
    unnamed x16 -> x24, local copies, waits for them, and re-layouts: 41.5 us -> 9.37 us
    dynamic_slice x33 -> x0, local copies, waits for them, and re-layouts: 29.7 us -> none  [the longest x32 29.7 us: in_blocks(): lax.scan(advance, carried, (jnp.arange(number, dtype=jnp.int32), stacked))]
    convert_element_type x2 -> x0, local copies, waits for them, and re-layouts: 12.7 us -> none  [encode(): return limited.astype(jnp.bfloat16).reshape(rows.shape[0], kv_local * HEAD)]
    another operation x2 -> x0, loops' own time: 11.7 us -> none  [in_blocks(): lax.scan(advance, carried, (jnp.arange(number, dtype=jnp.int32), stacked))]
  transfers between devices with their start and end apart: 2 -> 0, of which waited for: 2 -> 0; matrix products, arithmetic and copies ran while one was open for 1% -> 0% of each run, Pallas kernels for 0% -> 0%
where the time goes in v1:
time: 66.3 us; the launch traced here: 65.8 us
  Pallas kernels  55.8 us (84%)
  local copies, waits for them, and re-layouts  9.37 us (14%)
    pallas_call x1, Pallas kernels, local(): pl.pallas_call(kernel, out_shape=(jax.ShapeDtypeStruct(q.shape, BF), jax....  55.8 us
    unnamed x24, local copies, waits for them, and re-layouts  9.37 us

profile of v1, /device:TPU:1, one launch (start us, length us, event | category | flops | bytes accessed | tf_op | source)
XLA Modules:
  0.0 65.8 jit_solution(3452386395202320771)
XLA Ops:
  0.6 0.0 copy-start
  0.6 0.9 %copy-done = bf16[64,2048]{1,0:T(8,128)(2,1)S(1)} copy-done((bf16[64,2048]{1,0:T(8,128)(2,1)S(1)}, bf16[64,2048]{1,0:T(8,128)(2,1)}, u32[]{:S(2)}) %copy-start) | copy-done | bytes 262168
  1.6 0.0 copy-start.1
  1.6 0.8 %copy-done.1 = bf16[64,256]{1,0:T(8,128)(2,1)S(1)} copy-done((bf16[64,256]{1,0:T(8,128)(2,1)S(1)}, bf16[64,256]{1,0:T(8,128)(2,1)}, u32[]{:S(2)}) %copy-start.1) | copy-done | bytes 32792
  2.3 0.0 copy-start.2
  2.3 0.8 %copy-done.2 = bf16[64,256]{1,0:T(8,128)(2,1)S(1)} copy-done((bf16[64,256]{1,0:T(8,128)(2,1)S(1)}, bf16[64,256]{1,0:T(8,128)(2,1)}, u32[]{:S(2)}) %copy-start.2) | copy-done | bytes 32792
  3.1 0.0 copy-start.3
  3.1 0.8 %copy-done.3 = s32[128,128]{1,0:T(8,128)S(1)} copy-done((s32[128,128]{1,0:T(8,128)S(1)}, s32[128,128]{1,0:T(8,128)}, u32[]{:S(2)}) %copy-start.3) | copy-done | bytes 65560
  3.9 0.0 copy-start.4
  3.9 0.8 %copy-done.4 = bf16[4,2,2048]{2,1,0:T(2,128)(2,1)S(1)} copy-done((bf16[4,2,2048]{2,1,0:T(2,128)(2,1)S(1)}, bf16[4,2,2048]{2,1,0:T(2,128)(2,1)}, u32[]{:S(2)}) %copy-start.4) | copy-done | bytes 32792
  4.7 0.0 copy-start.5
  4.7 0.7 %copy-done.5 = bf16[4,2,256]{2,1,0:T(2,128)(2,1)S(1)} copy-done((bf16[4,2,256]{2,1,0:T(2,128)(2,1)S(1)}, bf16[4,2,256]{2,1,0:T(2,128)(2,1)}, u32[]{:S(2)}) %copy-start.5) | copy-done | bytes 4120
  5.4 0.0 copy-start.6
  5.4 0.7 %copy-done.6 = bf16[4,2,256]{2,1,0:T(2,128)(2,1)S(1)} copy-done((bf16[4,2,256]{2,1,0:T(2,128)(2,1)S(1)}, bf16[4,2,256]{2,1,0:T(2,128)(2,1)}, u32[]{:S(2)}) %copy-start.6) | copy-done | bytes 4120
  6.1 0.0 copy-start.7
  6.1 0.7 copy-done.7
  6.7 0.0 copy-start.8
  6.7 0.7 copy-done.8
  7.4 0.0 copy-start.9
  7.4 0.7 copy-done.9
  8.0 0.0 copy-start.10
  8.0 0.7 copy-done.10
  8.7 55.8 %shard_map.122 = (bf16[64,2048]{1,0:T(8,128)(2,1)S(1)}, bf16[4,2,2048]{2,1,0:T(2,128)(2,1)S(1)}) custom-call(s32[64]{0:T(128)S(1)} %copy-done.10, s32[2]{0:T(128)S(1)} %copy-done.7, s32[2]{0:T(128)S(1)} %copy-done.8, s32[2]{0:T(128)S(1)} %copy-done.9, bf16[64,2048]{1,0:T(8,128)(2,1)S(1)} %copy-done, bf16[64,256]{1,0:T(8,128)(2,1)S(1)} %copy-done.1, ...), custom_call_target="tpu_custom_call" | custom-call | tf_op jit(solution)/shard_map/pallas_call | solution.py:455
  64.5 0.7 %copy.15 = bf16[64,2048]{1,0:T(8,128)(2,1)} copy(bf16[64,2048]{1,0:T(8,128)(2,1)S(1)} %get-tuple-element.4) | data formatting | bytes 524288
  65.2 0.6 copy.16
Async XLA Ops:
  0.6 1.0 %copy-start = (bf16[64,2048]{1,0:T(8,128)(2,1)S(1)}, bf16[64,2048]{1,0:T(8,128)(2,1)}, u32[]{:S(2)}) copy-start(bf16[64,2048]{1,0:T(8,128)(2,1)} %q_ref.1) | copy-start | bytes 786436
  1.6 0.8 %copy-start.1 = (bf16[64,256]{1,0:T(8,128)(2,1)S(1)}, bf16[64,256]{1,0:T(8,128)(2,1)}, u32[]{:S(2)}) copy-start(bf16[64,256]{1,0:T(8,128)(2,1)} %k_own.1) | copy-start | bytes 98308
  2.3 0.8 %copy-start.2 = (bf16[64,256]{1,0:T(8,128)(2,1)S(1)}, bf16[64,256]{1,0:T(8,128)(2,1)}, u32[]{:S(2)}) copy-start(bf16[64,256]{1,0:T(8,128)(2,1)} %v_own.1) | copy-start | bytes 98308
  3.1 0.8 %copy-start.3 = (s32[128,128]{1,0:T(8,128)S(1)}, s32[128,128]{1,0:T(8,128)}, u32[]{:S(2)}) copy-start(s32[128,128]{1,0:T(8,128)} %mask_ref.1) | copy-start | bytes 196612
  3.9 0.8 %copy-start.4 = (bf16[4,2,2048]{2,1,0:T(2,128)(2,1)S(1)}, bf16[4,2,2048]{2,1,0:T(2,128)(2,1)}, u32[]{:S(2)}) copy-start(bf16[4,2,2048]{2,1,0:T(2,128)(2,1)} %dq_ref.1) | copy-start | bytes 98308
  4.7 0.7 %copy-start.5 = (bf16[4,2,256]{2,1,0:T(2,128)(2,1)S(1)}, bf16[4,2,256]{2,1,0:T(2,128)(2,1)}, u32[]{:S(2)}) copy-start(bf16[4,2,256]{2,1,0:T(2,128)(2,1)} %nk_ref.1) | copy-start | bytes 12292
  5.4 0.7 %copy-start.6 = (bf16[4,2,256]{2,1,0:T(2,128)(2,1)S(1)}, bf16[4,2,256]{2,1,0:T(2,128)(2,1)}, u32[]{:S(2)}) copy-start(bf16[4,2,256]{2,1,0:T(2,128)(2,1)} %nv_ref.1) | copy-start | bytes 12292
  6.1 0.7 copy-start.7
  6.7 0.7 copy-start.8
  7.4 0.7 copy-start.9
  8.0 0.7 copy-start.10

commit v2 on v1

--- a/solution.py
+++ b/solution.py
@@ -2,7 +2,6 @@
 
 import jax
 import jax.numpy as jnp
-import numpy as np
 from jax import lax
 from jax.experimental import pallas as pl
 from jax.experimental.pallas import tpu as pltpu
@@ -17,8 +16,7 @@
 ROWS = 2
 XS, ZS = 4, 8
 HALF = TOK // 2
-UNIT = 2 * HALF
-TILE = 512
+TILE = 256
 VERY_LOW = -1e30
 EPS = 1e-6
 WIDE = HEADS * HEAD
@@ -29,50 +27,78 @@
 MESH = pl.DeviceIdType.MESH
 
 OFFSETS = [(dx, dz) for dx in (0, -1, 1, 2) for dz in (0, -1, 1, -2, 2, -3, 3, 4)]
-WAVES = [[o for o in OFFSETS if abs(o[0]) + abs(o[1]) == d] for d in range(7)]
+ORDER = [(0, 0), (1, 0), (0, 1), (2, 0), (1, 1), (3, 0), (2, 1), (4, 0), (3, 1), (5, 0), (4, 1), (6, 0), (5, 1), (6, 1)]
+NW = len(ORDER)
+
+
+def sort_key(path, side):
+    far = -9 if side == 0 else 9
+
+    def key(off):
+        dx, dz = off
+        kx = far if dx == 2 else dx
+        kz = far if dz == 4 else dz
+        return (kz, kx) if path == 0 else (kx, kz)
+
+    return key
+
+
+UNITS = {}
 SLOT = {}
 START = []
-for wave in WAVES:
-    START.append(len(SLOT) * UNIT)
+for index, (d, side) in enumerate(ORDER):
+    START.append(len(SLOT) * HALF)
     for path in (0, 1):
-        for off in wave:
-            SLOT[(path, *off)] = len(SLOT)
-START.append(len(SLOT) * UNIT)
+        units = sorted(
+            (o for o in OFFSETS if abs(o[0]) + abs(o[1]) == d), key=sort_key(path, side)
+        )
+        UNITS[(index, path)] = units
+        for off in units:
+            SLOT[(side, path, *off)] = len(SLOT)
+START.append(len(SLOT) * HALF)
 OWN = START[-1]
 NTILE = OWN // TILE
-FIRST = [max(0, (START[d] // TILE)) for d in range(7)]
-TABLE = np.array(
-    [path * 64 + (dx % XS) * 8 + dz % ZS for (path, dx, dz) in SLOT], np.int32
-)
-
-
-def x_moves(dx):
-    return {
-        0: [("x", 1, -1, None), ("x", -1, 1, None)],
-        -1: [("x", 1, 2, 0)],
-        1: [("x", -1, 2, 1)],
-        2: [],
-    }[dx]
-
-
-def z_moves(dz):
-    if dz == 0:
-        return [("z", 1, -1, None), ("z", -1, 1, None)]
-    if dz == 4:
+NEED = [max(k for k in range(NW) if START[k] < (t + 1) * TILE) for t in range(NTILE)]
+AFTER = {k: ORDER.index((d + 1, side)) for k, (d, side) in enumerate(ORDER) if d < 6}
+TABLE = [
+    side * 128 + path * 64 + (dx % XS) * 8 + dz % ZS for (side, path, dx, dz) in SLOT
+]
+
+
+def hops(n, far, side):
+    if n == 0:
+        return [(1, -1), (-1, 1)]
+    if n == far:
         return []
-    way = 1 if dz < 0 else -1
-    if abs(dz) == 3:
-        return [("z", way, 4, 0 if dz < 0 else 1)]
-    return [("z", way, dz - way, None)]
-
-
-def moves(path, dx, dz):
+    way = 1 if n < 0 else -1
+    if abs(n) == far - 1:
+        return [(way, far)] if (way == 1) == (side == 0) else []
+    return [(way, n - way)]
+
+
+def messages(k):
+    side = ORDER[k][1]
     out = []
-    if path == 0 or dx == 0:
-        out += [(a, w, SLOT[(path, dx, n)], h) for a, w, n, h in z_moves(dz)]
-    if path == 1 or dz == 0:
-        out += [(a, w, SLOT[(path, n, dz)], h) for a, w, n, h in x_moves(dx)]
-    return out
+    for path in (0, 1):
+        for dx, dz in UNITS[(k, path)]:
+            here = SLOT[(side, path, dx, dz)] * HALF
+            if path == 0 or dx == 0:
+                for way, n in hops(dz, 4, side):
+                    out.append((path, "z", way, here, SLOT[(side, path, dx, n)] * HALF))
+            if path == 1 or dz == 0:
+                for way, n in hops(dx, 2, side):
+                    out.append((path, "x", way, here, SLOT[(side, path, n, dz)] * HALF))
+    out.sort(key=lambda m: (m[0], m[1], m[2], m[3]))
+    merged = []
+    for path, axis, way, here, there in out:
+        if merged:
+            p, a, w, h, t, n = merged[-1]
+            if (p, a, w) == (path, axis, way) and h + n == here and t + n == there:
+                merged[-1] = (p, a, w, h, t, n + HALF)
+                continue
+        merged.append((path, axis, way, here, there, HALF))
+    merged.sort(key=lambda m: m[0] if m[1] == "z" else 1 - m[0])
+    return [m[1:] for m in merged]
 
 
 def dot(a, b):
@@ -87,21 +113,27 @@
 
 
 def kernel(
+    q_hbm,
+    k_hbm,
+    v_hbm,
+    mask_hbm,
+    widths_hbm,
+    exps_hbm,
+    dq_hbm,
+    nk_hbm,
+    nv_hbm,
+    ctx_hbm,
+    out_ref,
+    dout_ref,
     table,
     widths,
     exps,
     ctx,
     q_ref,
-    k_hbm,
-    v_hbm,
-    k_own,
-    v_own,
     mask_ref,
     dq_ref,
     nk_ref,
     nv_ref,
-    out_ref,
-    dout_ref,
     kv,
     qx,
     qd,
@@ -125,7 +157,6 @@
     sq_theirs,
     load_sem,
     y_send,
-    y_recv,
     send_sem,
     recv_sem,
     sib_send,
@@ -152,26 +183,30 @@
     across = at(1 - yh, x, z, core)
     sibling = at(yh, x, z, 1 - core)
 
-    loads = []
-    for path in (0, 1):
-        for part, src in enumerate((k_hbm, v_hbm)):
-            loads.append(
-                pltpu.make_async_copy(
-                    src.at[pl.ds(path * HALF, HALF), :],
-                    kv.at[pl.ds(path * UNIT + yh * HALF, HALF), pl.ds(part * 256, 256)],
-                    load_sem.at[path * 2 + part],
-                )
-            )
-    for c in loads:
-        c.start()
-
     barrier = pltpu.get_barrier_semaphore()
     for dev in (*peers.values(), across, sibling):
         pl.semaphore_signal(barrier, inc=1, device_id=(dev, grp), device_id_type=MESH)
     pl.semaphore_signal(barrier, inc=1, device_id=(s, 1 - grp), device_id_type=MESH)
+
+    loads = [
+        pltpu.make_async_copy(src, dst, load_sem.at[i])
+        for i, (src, dst) in enumerate(
+            (
+                (k_hbm, kv.at[pl.ds(0, TOK), pl.ds(0, 256)]),
+                (v_hbm, kv.at[pl.ds(0, TOK), pl.ds(256, 256)]),
+                (q_hbm, q_ref),
+                (mask_hbm, mask_ref),
+                (widths_hbm, widths),
+                (exps_hbm, exps),
+                (ctx_hbm, ctx),
+                (dq_hbm, dq_ref),
+                (nk_hbm, nk_ref),
+                (nv_hbm, nv_ref),
+            )
+        )
+    ]
     for c in loads:
-        c.wait()
-    pl.semaphore_wait(barrier, 7)
+        c.start()
 
     def remote(src_row, dst_row, count, ssem, rsem, dev):
         return pltpu.make_async_remote_copy(
@@ -183,12 +218,41 @@
             device_id_type=MESH,
         )
 
-    ycopies = []
-    for path in (0, 1):
-        row = path * UNIT + yh * HALF
-        ycopies.append(remote(row, row, HALF, y_send.at[path], y_recv.at[path], across))
-    for c in ycopies:
-        c.start()
+    def forwards(k):
+        if k in AFTER:
+            n = AFTER[k]
+            for axis, way, here, there, count in messages(k):
+                remote(
+                    here, there, count, send_sem.at[n], recv_sem.at[n], peers[(axis, way)]
+                ).start()
+
+    def wave_copy(k):
+        return remote(
+            START[k], START[k], START[k + 1] - START[k], send_sem.at[k], recv_sem.at[k], sibling
+        )
+
+    def to_sibling(k):
+        return remote(
+            START[k],
+            OWN + START[k],
+            START[k + 1] - START[k],
+            sib_send.at[k],
+            sib_recv.at[k],
+            sibling,
+        )
+
+    other = ORDER.index((0, 1))
+    ycopy = remote(0, START[other], TOK, y_send, recv_sem.at[other], across)
+    loads[0].wait()
+    loads[1].wait()
+    pl.semaphore_wait(barrier, 7)
+    ycopy.start()
+    forwards(0)
+    to_sibling(0).start()
+    for i, code in enumerate(TABLE):
+        table[i] = code
+    for c in loads[2:]:
+        c.wait()
 
     i0 = lax.broadcasted_iota(jnp.int32, (256, 256), 0)
     i1 = lax.broadcasted_iota(jnp.int32, (256, 256), 1)
@@ -224,13 +288,13 @@
             else:
                 two = jnp.concatenate([held, whole], axis=0)
                 qx[kh, :, (g - 1) * TOK : (g + 1) * TOK] = two.T.astype(BF)
-        sc = dot(k_own[:, kh * HEAD : (kh + 1) * HEAD], qx[kh, 0:128, :])
+        sc = dot(kv[0:TOK, kh * HEAD : (kh + 1) * HEAD], qx[kh, 0:128, :])
         sc = jnp.where(tri, sc, VERY_LOW)
         top = jnp.max(sc, axis=0, keepdims=True)
         w = jnp.exp2((sc - top) * SCORE)
         m_p[kh] = top
         l_p[kh] = jnp.sum(w, axis=0, keepdims=True)
-        vt = v_own[:, kh * HEAD : (kh + 1) * HEAD].astype(F32).T.astype(BF)
+        vt = kv[0:TOK, 256 + kh * HEAD : 256 + (kh + 1) * HEAD].astype(F32).T.astype(BF)
         o_p[kh] = dot(vt, w.astype(BF))
 
     for h in range(KV * GROUP):
@@ -277,74 +341,40 @@
     o_0[...] = jnp.where(first_head, wide[0:128], wide[128:256])
     o_d[...] = jnp.zeros_like(o_d)
 
-    def forwards(d):
-        for path in (0, 1):
-            for dx, dz in WAVES[d]:
-                here = SLOT[(path, dx, dz)] * UNIT
-                for axis, way, there, half in moves(path, dx, dz):
-                    shift, count = (0, UNIT) if half is None else (half * HALF, HALF)
-                    remote(
-                        here + shift,
-                        there * UNIT + shift,
-                        count,
-                        send_sem.at[d + 1],
-                        recv_sem.at[d + 1],
-                        peers[(axis, way)],
-                    ).start()
-
-    def wave_copy(d):
-        return remote(
-            START[d], START[d], START[d + 1] - START[d], send_sem.at[d], recv_sem.at[d], sibling
-        )
-
-    def to_sibling(d):
-        return remote(
-            START[d],
-            OWN + START[d],
-            START[d + 1] - START[d],
-            sib_send.at[d],
-            sib_recv.at[d],
-            sibling,
-        )
-
-    for c in ycopies:
-        c.wait_recv()
-    forwards(0)
-    to_sibling(0).start()
-
     def step(i, carry):
-        for d in range(1, 7):
-            at_step = 2 * max(FIRST[d], 0) if d > 1 else 0
-            if d in (2,):
-                at_step = 2 * 1
-
-            @pl.when(i == at_step)
+        done = 0
+        for t in range(NTILE):
+            waves = range(done + 1, NEED[t] + 1)
+            sent = range(done + 1 if t else 0, NEED[t] + 1)
+            done = NEED[t]
+            if not sent:
+                continue
+
+            @pl.when(i == 2 * t)
             def _():
-                wave_copy(d).wait_recv()
-                if d < 6:
-                    forwards(d)
-                to_sibling(d).start()
-
-            @pl.when(i == at_step + 1)
+                for k in waves:
+                    wave_copy(k).wait_recv()
+                    forwards(k)
+                    to_sibling(k).start()
+
+            @pl.when(i == 2 * t + 1)
             def _():
-                if d == 1:
-                    to_sibling(0).wait_recv()
-                to_sibling(d).wait_recv()
+                for k in sent:
+                    to_sibling(k).wait_recv()
 
         e = i % 2
         tile = i // 2
         first = pl.multiple_of(e * OWN + tile * TILE, TILE)
         rows_in = lax.broadcasted_iota(jnp.int32, (HALF, 128), 0)
         lanes_in = lax.broadcasted_iota(jnp.int32, (HALF, 128), 1)
-        for u in range(TILE // UNIT):
-            code = table[tile * (TILE // UNIT) + u]
+        for u in range(TILE // HALF):
+            code = table[tile * (TILE // HALF) + u]
             sx = (x + (code % 64) // 8) % XS
             sz = (z + code % 8) % ZS
-            for y in (0, 1):
-                block = at(y, sx, sz, (core + e) % 2)
-                here = slice(u * UNIT + y * HALF, u * UNIT + (y + 1) * HALF)
-                oh[here, :] = jnp.where(lanes_in == block, 1.0, 0.0).astype(BF)
-                pos[here, :] = rows_in + (block * TOK + (code // 64) * HALF)
+            block = at((yh + code // 128) % 2, sx, sz, (core + e) % 2)
+            here = slice(u * HALF, (u + 1) * HALF)
+            oh[here, :] = jnp.where(lanes_in == block, 1.0, 0.0).astype(BF)
+            pos[here, :] = rows_in + (block * TOK + (code // 64) % 2 * HALF)
 
         keys = kv[pl.ds(first, TILE), 0:256]
         vals_t = kv[pl.ds(first, TILE), 256:512].T
@@ -428,12 +458,11 @@
     )
     swap.start()
 
-    for c in ycopies:
-        c.wait_send()
-    for d in range(7):
-        if d > 0:
-            wave_copy(d).wait_send()
-        to_sibling(d).wait_send()
+    ycopy.wait_send()
+    for k in range(NW):
+        if ORDER[k][0] > 0:
+            wave_copy(k).wait_send()
+        to_sibling(k).wait_send()
     swap.wait()
     norm = lax.rsqrt((sq_mine[...] + sq_theirs[...]) / WIDE + EPS)
     for kh in range(KV):
@@ -449,8 +478,7 @@
 
 def local(q, k, v, mask, widths, exps, dq, nk, nv, ctx):
     vmem = pl.BlockSpec(memory_space=pltpu.VMEM)
-    smem = pl.BlockSpec(memory_space=pltpu.SMEM)
-    anyw = pl.BlockSpec(memory_space=pl.ANY)
+    hbm = pl.BlockSpec(memory_space=pltpu.HBM)
     dma = pltpu.SemaphoreType.DMA
     return pl.pallas_call(
         kernel,
@@ -458,9 +486,18 @@
             jax.ShapeDtypeStruct(q.shape, BF),
             jax.ShapeDtypeStruct(dq.shape, BF),
         ),
-        in_specs=[smem] * 4 + [vmem, anyw, anyw] + [vmem] * 6,
+        in_specs=[hbm] * 10,
         out_specs=(vmem, vmem),
         scratch_shapes=[
+            pltpu.SMEM((len(TABLE),), jnp.int32),
+            pltpu.SMEM((KV,), jnp.int32),
+            pltpu.SMEM((KV,), jnp.int32),
+            pltpu.SMEM((ROWS,), jnp.int32),
+            pltpu.VMEM(q.shape, BF),
+            pltpu.VMEM(mask.shape, jnp.int32),
+            pltpu.VMEM(dq.shape, BF),
+            pltpu.VMEM(nk.shape, BF),
+            pltpu.VMEM(nv.shape, BF),
             pltpu.VMEM((2 * OWN, 512), BF),
             pltpu.VMEM((KV, 256, 512), BF),
             pltpu.VMEM((256, 256), BF),
@@ -482,20 +519,19 @@
             pltpu.VMEM((128, 128), F32),
             pltpu.VMEM((TOK + 8, 128), F32),
             pltpu.VMEM((TOK + 8, 128), F32),
-            dma((4,)),
-            dma((2,)),
-            dma((2,)),
-            dma((7,)),
-            dma((7,)),
-            dma((7,)),
-            dma((7,)),
+            dma((10,)),
+            dma,
+            dma((NW,)),
+            dma((NW,)),
+            dma((NW,)),
+            dma((NW,)),
             dma,
             dma,
         ],
         compiler_params=pltpu.CompilerParams(
             collective_id=0, has_side_effects=True, vmem_limit_bytes=48 * 1024 * 1024
         ),
-    )(jnp.asarray(TABLE), widths, exps, ctx, q, k, v, k, v, mask, dq, nk, nv)
+    )(q, k, v, mask, widths, exps, dq, nk, nv, ctx)
 
 
 def solution(mesh):

time: 66.3 us -> 86.2 us (1.30)
  Pallas kernels: 55.8 us -> 76.4 us
    pallas_call x1, Pallas kernels: 55.8 us -> 76.4 us  [local(): pl.pallas_call(kernel, out_shape=(jax.ShapeDtypeStruct(q.shape, BF), jax....]
    unnamed x24 -> x22, local copies, waits for them, and re-layouts: 9.37 us -> 8.71 us
where the time goes in v2:
time: 86.2 us; the launch traced here: 85.8 us
  Pallas kernels  76.4 us (89%)
  local copies, waits for them, and re-layouts  8.71 us (10%)
    pallas_call x1, Pallas kernels, local(): pl.pallas_call(kernel, out_shape=(jax.ShapeDtypeStruct(q.shape, BF), jax....  76.4 us
    unnamed x22, local copies, waits for them, and re-layouts  8.71 us

profile of v2, /device:TPU:1, one launch (start us, length us, event | category | flops | bytes accessed | tf_op | source)
XLA Modules:
  0.0 85.8 jit_solution(8297350027421310149)
XLA Ops:
  0.6 0.0 copy-start
  0.6 0.9 %copy-done = bf16[64,2048]{1,0:T(8,128)(2,1)S(1)} copy-done((bf16[64,2048]{1,0:T(8,128)(2,1)S(1)}, bf16[64,2048]{1,0:T(8,128)(2,1)}, u32[]{:S(2)}) %copy-start) | copy-done | bytes 262168
  1.6 0.0 copy-start.1
  1.6 0.8 copy-done.1
  2.4 0.0 copy-start.2
  2.4 0.8 copy-done.2
  3.2 0.0 copy-start.3
  3.2 0.8 copy-done.3
  3.9 0.0 copy-start.4
  3.9 0.8 copy-done.4
  4.7 0.0 copy-start.5
  4.7 0.7 copy-done.5
  5.4 0.0 copy-start.6
  5.4 0.7 copy-done.6
  6.1 0.0 copy-start.7
  6.1 0.7 copy-done.7
  6.7 0.0 copy-start.8
  6.7 0.7 copy-done.8
  7.4 0.0 copy-start.9
  7.4 0.7 copy-done.9
  8.0 76.4 %shard_map.113 = (bf16[64,2048]{1,0:T(8,128)(2,1)S(1)}, bf16[4,2,2048]{2,1,0:T(2,128)(2,1)S(1)}) custom-call(bf16[64,2048]{1,0:T(8,128)(2,1)S(1)} %copy-done, bf16[64,256]{1,0:T(8,128)(2,1)S(1)} %copy-done.2, bf16[64,256]{1,0:T(8,128)(2,1)S(1)} %copy-done.3, s32[128,128]{1,0:T(8,128)S(1)} %copy-done.1, s32[2]{0:T(128)S(1)} %copy-done.7, s32[2]{0:T(128)S(1)} %copy-done.8, ...), custom_call_target="tpu_custom_call" | custom-call | tf_op jit(solution)/shard_map/pallas_call | solution.py:483
  84.4 0.7 copy.14
  85.1 0.6 copy.15
Async XLA Ops:
  0.6 1.0 %copy-start = (bf16[64,2048]{1,0:T(8,128)(2,1)S(1)}, bf16[64,2048]{1,0:T(8,128)(2,1)}, u32[]{:S(2)}) copy-start(bf16[64,2048]{1,0:T(8,128)(2,1)} %q_hbm.1) | copy-start | bytes 786436
  1.6 0.8 copy-start.1
  2.4 0.8 copy-start.2
  3.2 0.8 copy-start.3
  3.9 0.8 copy-start.4
  4.7 0.7 copy-start.5
  5.4 0.7 copy-start.6
  6.1 0.7 copy-start.7
  6.7 0.7 copy-start.8
  7.4 0.7 copy-start.9

commit v3 on v2

--- a/solution.py
+++ b/solution.py
@@ -16,7 +16,7 @@
 ROWS = 2
 XS, ZS = 4, 8
 HALF = TOK // 2
-TILE = 256
+TILE = 512
 VERY_LOW = -1e30
 EPS = 1e-6
 WIDE = HEADS * HEAD
@@ -341,29 +341,7 @@
     o_0[...] = jnp.where(first_head, wide[0:128], wide[128:256])
     o_d[...] = jnp.zeros_like(o_d)
 
-    def step(i, carry):
-        done = 0
-        for t in range(NTILE):
-            waves = range(done + 1, NEED[t] + 1)
-            sent = range(done + 1 if t else 0, NEED[t] + 1)
-            done = NEED[t]
-            if not sent:
-                continue
-
-            @pl.when(i == 2 * t)
-            def _():
-                for k in waves:
-                    wave_copy(k).wait_recv()
-                    forwards(k)
-                    to_sibling(k).start()
-
-            @pl.when(i == 2 * t + 1)
-            def _():
-                for k in sent:
-                    to_sibling(k).wait_recv()
-
-        e = i % 2
-        tile = i // 2
+    def compute(e, tile):
         first = pl.multiple_of(e * OWN + tile * TILE, TILE)
         rows_in = lax.broadcasted_iota(jnp.int32, (HALF, 128), 0)
         lanes_in = lax.broadcasted_iota(jnp.int32, (HALF, 128), 1)
@@ -423,9 +401,26 @@
             axis=0,
         )
         o_d[...] = o_d[...] * fade + dot(coded, w.astype(BF))
-        return carry
-
-    lax.fori_loop(0, 2 * NTILE, step, 0)
+
+    for k in range(1, NW + 1):
+        if k < NW:
+            wave_copy(k).wait_recv()
+            forwards(k)
+            to_sibling(k).start()
+        to_sibling(k - 1).wait_recv()
+        mine = [t for t in range(NTILE) if NEED[t] == k]
+        theirs = [t for t in range(NTILE) if NEED[t] == k - 1]
+        n_theirs, n_all = len(theirs), len(theirs) + len(mine)
+        if not n_all:
+            continue
+        t_theirs, t_mine = (theirs or [0])[0], (mine or [0])[0]
+
+        def step(j, carry):
+            e = jnp.where(j < n_theirs, 1, 0)
+            compute(e, jnp.where(j < n_theirs, t_theirs + j, t_mine + j - n_theirs))
+            return carry
+
+        lax.fori_loop(0, n_all, step, 0)
 
     turned = jnp.where(first_head, o_d[0:128, :], o_d[128:256, :])
     high = turned.astype(BF)
@@ -529,7 +524,7 @@
             dma,
         ],
         compiler_params=pltpu.CompilerParams(
-            collective_id=0, has_side_effects=True, vmem_limit_bytes=48 * 1024 * 1024
+            collective_id=0, has_side_effects=True, vmem_limit_bytes=67_043_328
         ),
     )(q, k, v, mask, widths, exps, dq, nk, nv, ctx)
 

time: 86.2 us -> 60.5 us (0.70)
  Pallas kernels: 76.4 us -> 56.9 us
  local copies, waits for them, and re-layouts: 8.71 us -> 2.29 us
    pallas_call x1, Pallas kernels: 76.4 us -> 56.9 us  [local(): pl.pallas_call(kernel, out_shape=(jax.ShapeDtypeStruct(q.shape, BF), jax....]
    unnamed x22 -> x4, local copies, waits for them, and re-layouts: 8.71 us -> 2.29 us
where the time goes in v3:
time: 60.5 us; the launch traced here: 59.8 us
  Pallas kernels  56.9 us (94%)
  local copies, waits for them, and re-layouts  2.29 us (4%)
  between operations  0.65 us (1%)
    pallas_call x1, Pallas kernels, local(): pl.pallas_call(kernel, out_shape=(jax.ShapeDtypeStruct(q.shape, BF), jax....  56.9 us
    unnamed x4, local copies, waits for them, and re-layouts  2.29 us

profile of v3, /device:TPU:1, one launch (start us, length us, event | category | flops | bytes accessed | tf_op | source)
XLA Modules:
  0.0 59.8 jit_solution(10453737621842006258)
XLA Ops:
  0.6 56.9 %shard_map.113 = (bf16[64,2048]{1,0:T(8,128)(2,1)}, bf16[4,2,2048]{2,1,0:T(2,128)(2,1)}) custom-call(bf16[64,2048]{1,0:T(8,128)(2,1)} %q_hbm.1, bf16[64,256]{1,0:T(8,128)(2,1)} %k_hbm.1, bf16[64,256]{1,0:T(8,128)(2,1)} %v_hbm.1, s32[128,128]{1,0:T(8,128)} %mask_hbm.1, s32[2]{0:T(128)} %widths_hbm.1, s32[2]{0:T(128)} %exps_hbm.1, bf16[4,2,2048]{2,1,0:T(2,128)(2,1)} %dq_hbm.1, ...), custom_call_target="tpu_custom_call" | custom-call | tf_op jit(solution)/shard_map/pallas_call | solution.py:478
  57.5 0.0 copy-start
  57.5 1.7 %copy.14 = bf16[64,2048]{1,0:T(8,128)(2,1)} copy(bf16[64,2048]{1,0:T(8,128)(2,1)} %get-tuple-element.4) | data formatting | bytes 524288
  59.2 0.0 copy-done
  59.2 0.6 %copy.15 = bf16[4,2,2048]{2,1,0:T(2,128)(2,1)} copy(bf16[4,2,2048]{2,1,0:T(2,128)(2,1)S(1)} %copy-done) | data formatting | bytes 65536
Async XLA Ops:
  57.5 1.7 %copy-start = (bf16[4,2,2048]{2,1,0:T(2,128)(2,1)S(1)}, bf16[4,2,2048]{2,1,0:T(2,128)(2,1)}, u32[]{:S(2)}) copy-start(bf16[4,2,2048]{2,1,0:T(2,128)(2,1)} %get-tuple-element.5) | copy-start | bytes 98308

commit v4 on v3

--- a/solution.py
+++ b/solution.py
@@ -26,9 +26,39 @@
 F32 = jnp.float32
 MESH = pl.DeviceIdType.MESH
 
+PLAN = [
+    ((0, 0, 0), []),
+    ((0, 0, 1), []),
+    ((1, 0, 0), []),
+    ((1, 0, 1), []),
+    ((0, 1, 0), []),
+    ((0, 1, 1), []),
+    ((2, 0, 0), [(0, 0)]),
+    ((2, 0, 1), []),
+    ((1, 1, 0), [(1, 0)]),
+    ((1, 1, 1), [(0, 1), (1, 1)]),
+    ((3, 0, 0), []),
+    ((3, 0, 1), [(0, 2)]),
+    ((2, 1, 0), []),
+    ((2, 1, 1), [(1, 2), (0, 3), (1, 3)]),
+    ((4, 0, 0), []),
+    ((4, 0, 1), []),
+    ((3, 1, 0), [(0, 4)]),
+    ((3, 1, 1), [(1, 4)]),
+    ((5, 0, 1), []),
+    ((5, 0, 0), [(0, 5), (1, 5)]),
+    ((4, 1, 0), []),
+    ((6, 0, 1), []),
+    ((4, 1, 1), []),
+    ((6, 0, 0), [(0, 6), (1, 6)]),
+    ((5, 1, 0), []),
+    ((5, 1, 1), []),
+    ((6, 1, 0), []),
+    ((6, 1, 1), [(0, 7), (1, 7)]),
+]
+ORDER = [g for g, _ in PLAN]
+NW = len(ORDER)
 OFFSETS = [(dx, dz) for dx in (0, -1, 1, 2) for dz in (0, -1, 1, -2, 2, -3, 3, 4)]
-ORDER = [(0, 0), (1, 0), (0, 1), (2, 0), (1, 1), (3, 0), (2, 1), (4, 0), (3, 1), (5, 0), (4, 1), (6, 0), (5, 1), (6, 1)]
-NW = len(ORDER)
 
 
 def sort_key(path, side):
@@ -43,26 +73,22 @@
     return key
 
 
-UNITS = {}
+UNITS = []
 SLOT = {}
 START = []
-for index, (d, side) in enumerate(ORDER):
+for d, side, path in ORDER:
     START.append(len(SLOT) * HALF)
-    for path in (0, 1):
-        units = sorted(
-            (o for o in OFFSETS if abs(o[0]) + abs(o[1]) == d), key=sort_key(path, side)
-        )
-        UNITS[(index, path)] = units
-        for off in units:
-            SLOT[(side, path, *off)] = len(SLOT)
+    UNITS.append(
+        sorted((o for o in OFFSETS if abs(o[0]) + abs(o[1]) == d), key=sort_key(path, side))
+    )
+    for off in UNITS[-1]:
+        SLOT[(side, path, *off)] = len(SLOT)
 START.append(len(SLOT) * HALF)
+SOURCES = list(SLOT)
 OWN = START[-1]
 NTILE = OWN // TILE
 NEED = [max(k for k in range(NW) if START[k] < (t + 1) * TILE) for t in range(NTILE)]
-AFTER = {k: ORDER.index((d + 1, side)) for k, (d, side) in enumerate(ORDER) if d < 6}
-TABLE = [
-    side * 128 + path * 64 + (dx % XS) * 8 + dz % ZS for (side, path, dx, dz) in SLOT
-]
+AFTER = {k: ORDER.index((d + 1, side, path)) for k, (d, side, path) in enumerate(ORDER) if d < 6}
 
 
 def hops(n, far, side):
@@ -77,17 +103,16 @@
 
 
 def messages(k):
-    side = ORDER[k][1]
+    _, side, path = ORDER[k]
     out = []
-    for path in (0, 1):
-        for dx, dz in UNITS[(k, path)]:
-            here = SLOT[(side, path, dx, dz)] * HALF
-            if path == 0 or dx == 0:
-                for way, n in hops(dz, 4, side):
-                    out.append((path, "z", way, here, SLOT[(side, path, dx, n)] * HALF))
-            if path == 1 or dz == 0:
-                for way, n in hops(dx, 2, side):
-                    out.append((path, "x", way, here, SLOT[(side, path, n, dz)] * HALF))
+    for dx, dz in UNITS[k]:
+        here = SLOT[(side, path, dx, dz)] * HALF
+        if path == 0 or dx == 0:
+            for way, n in hops(dz, 4, side):
+                out.append((path, "z", way, here, SLOT[(side, path, dx, n)] * HALF))
+        if path == 1 or dz == 0:
+            for way, n in hops(dx, 2, side):
+                out.append((path, "x", way, here, SLOT[(side, path, n, dz)] * HALF))
     out.sort(key=lambda m: (m[0], m[1], m[2], m[3]))
     merged = []
     for path, axis, way, here, there in out:
@@ -125,7 +150,6 @@
     ctx_hbm,
     out_ref,
     dout_ref,
-    table,
     widths,
     exps,
     ctx,
@@ -241,16 +265,19 @@
             sibling,
         )
 
-    other = ORDER.index((0, 1))
-    ycopy = remote(0, START[other], TOK, y_send, recv_sem.at[other], across)
+    theirs = [ORDER.index((0, 1, path)) for path in (0, 1)]
+    ycopies = [
+        remote(path * HALF, START[k], HALF, y_send.at[path], recv_sem.at[k], across)
+        for path, k in enumerate(theirs)
+    ]
     loads[0].wait()
     loads[1].wait()
     pl.semaphore_wait(barrier, 7)
-    ycopy.start()
-    forwards(0)
-    to_sibling(0).start()
-    for i, code in enumerate(TABLE):
-        table[i] = code
+    for c in ycopies:
+        c.start()
+    for k in (0, 1):
+        forwards(k)
+        to_sibling(k).start()
     for c in loads[2:]:
         c.wait()
 
@@ -341,25 +368,50 @@
     o_0[...] = jnp.where(first_head, wide[0:128], wide[128:256])
     o_d[...] = jnp.zeros_like(o_d)
 
+    rows_in = lax.broadcasted_iota(jnp.int32, (HALF, 128), 0)
+    lanes_in = lax.broadcasted_iota(jnp.int32, (HALF, 128), 1)
+    part_y = [at((yh + o) % 2, 0, 0, 0) for o in (0, 1)]
+    part_x = [at(0, (x + o) % XS, 0, 0) for o in range(XS)]
+    part_z = [at(0, 0, (z + o) % ZS, 0) for o in range(ZS)]
+    part_core = [(core + o) % 2 for o in (0, 1)]
+
     def compute(e, tile):
-        first = pl.multiple_of(e * OWN + tile * TILE, TILE)
-        rows_in = lax.broadcasted_iota(jnp.int32, (HALF, 128), 0)
-        lanes_in = lax.broadcasted_iota(jnp.int32, (HALF, 128), 1)
+        first = e * OWN + tile * TILE
         for u in range(TILE // HALF):
-            code = table[tile * (TILE // HALF) + u]
-            sx = (x + (code % 64) // 8) % XS
-            sz = (z + code % 8) % ZS
-            block = at((yh + code // 128) % 2, sx, sz, (core + e) % 2)
+            side, path, dx, dz = SOURCES[tile * (TILE // HALF) + u]
+            block = part_y[side] + part_x[dx % XS] + part_z[dz % ZS] + part_core[e]
             here = slice(u * HALF, (u + 1) * HALF)
             oh[here, :] = jnp.where(lanes_in == block, 1.0, 0.0).astype(BF)
-            pos[here, :] = rows_in + (block * TOK + (code // 64) % 2 * HALF)
+            pos[here, :] = rows_in + (block * TOK + path * HALF)
 
         keys = kv[pl.ds(first, TILE), 0:256]
+        blocks = oh[...]
+        scores = [
+            dot(
+                jnp.concatenate([keys[:, kh * HEAD : (kh + 1) * HEAD], blocks], axis=1), qx[kh]
+            )
+            for kh in range(KV)
+        ]
         vals_t = kv[pl.ds(first, TILE), 256:512].T
-        blocks = oh[...]
+
+        def code(rot, axis):
+            return jnp.concatenate(
+                [
+                    jnp.clip(
+                        jnp.floor(lax.slice_in_dim(rot, j * HEAD, (j + 1) * HEAD, axis=axis) * forward[j] + 0.5),
+                        -level[j],
+                        level[j],
+                    ).astype(BF)
+                    for j in range(KV)
+                ],
+                axis=axis,
+            )
+
+        coded_k = code(dot(keys, h2[...]), 1)
+        coded_v = code(dot(h2[...], vals_t), 0)
+        two = dot(coded_k, qd[...])
         for kh in range(KV):
-            ext = jnp.concatenate([keys[:, kh * HEAD : (kh + 1) * HEAD], blocks], axis=1)
-            sc = dot(ext, qx[kh])
+            sc = scores[kh]
             old = m_p[kh]
             top = jnp.maximum(old, jnp.max(sc, axis=0, keepdims=True))
             w = jnp.exp2(sc * SCORE - top * SCORE)
@@ -367,20 +419,6 @@
             m_p[kh] = top
             l_p[kh] = l_p[kh] * fade + jnp.sum(w, axis=0, keepdims=True)
             o_p[kh] = o_p[kh] * fade + dot(vals_t[kh * HEAD : (kh + 1) * HEAD, :], w.astype(BF))
-
-        rot = dot(keys, h2[...])
-        coded = jnp.concatenate(
-            [
-                jnp.clip(
-                    jnp.floor(rot[:, j * HEAD : (j + 1) * HEAD] * forward[j] + 0.5),
-                    -level[j],
-                    level[j],
-                ).astype(BF)
-                for j in range(KV)
-            ],
-            axis=1,
-        )
-        two = dot(coded, qd[...])
         sc = jnp.where(pos[...] < limits, two[:, 0:128] + two[:, 128:256], VERY_LOW)
         old = m_d[...]
         top = jnp.maximum(old, jnp.max(sc, axis=0, keepdims=True))
@@ -388,39 +426,20 @@
         fade = jnp.exp2((old - top) * SCORE)
         m_d[...] = top
         l_d[...] = l_d[...] * fade + jnp.sum(w, axis=0, keepdims=True)
-        rot = dot(h2[...], vals_t)
-        coded = jnp.concatenate(
-            [
-                jnp.clip(
-                    jnp.floor(rot[j * HEAD : (j + 1) * HEAD, :] * forward[j] + 0.5),
-                    -level[j],
-                    level[j],
-                ).astype(BF)
-                for j in range(KV)
-            ],
-            axis=0,
-        )
-        o_d[...] = o_d[...] * fade + dot(coded, w.astype(BF))
-
-    for k in range(1, NW + 1):
-        if k < NW:
+        o_d[...] = o_d[...] * fade + dot(coded_v, w.astype(BF))
+
+
+    shared = 0
+    for k, (_, tiles) in enumerate(PLAN):
+        if k > 1:
             wave_copy(k).wait_recv()
             forwards(k)
             to_sibling(k).start()
-        to_sibling(k - 1).wait_recv()
-        mine = [t for t in range(NTILE) if NEED[t] == k]
-        theirs = [t for t in range(NTILE) if NEED[t] == k - 1]
-        n_theirs, n_all = len(theirs), len(theirs) + len(mine)
-        if not n_all:
-            continue
-        t_theirs, t_mine = (theirs or [0])[0], (mine or [0])[0]
-
-        def step(j, carry):
-            e = jnp.where(j < n_theirs, 1, 0)
-            compute(e, jnp.where(j < n_theirs, t_theirs + j, t_mine + j - n_theirs))
-            return carry
-
-        lax.fori_loop(0, n_all, step, 0)
+        for e, t in tiles:
+            while e == 1 and shared <= NEED[t]:
+                to_sibling(shared).wait_recv()
+                shared += 1
+            compute(e, t)
 
     turned = jnp.where(first_head, o_d[0:128, :], o_d[128:256, :])
     high = turned.astype(BF)
@@ -453,7 +472,8 @@
     )
     swap.start()
 
-    ycopy.wait_send()
+    for c in ycopies:
+        c.wait_send()
     for k in range(NW):
         if ORDER[k][0] > 0:
             wave_copy(k).wait_send()
@@ -484,7 +504,6 @@
         in_specs=[hbm] * 10,
         out_specs=(vmem, vmem),
         scratch_shapes=[
-            pltpu.SMEM((len(TABLE),), jnp.int32),
             pltpu.SMEM((KV,), jnp.int32),
             pltpu.SMEM((KV,), jnp.int32),
             pltpu.SMEM((ROWS,), jnp.int32),
@@ -515,7 +534,7 @@
             pltpu.VMEM((TOK + 8, 128), F32),
             pltpu.VMEM((TOK + 8, 128), F32),
             dma((10,)),
-            dma,
+            dma((2,)),
             dma((NW,)),
             dma((NW,)),
             dma((NW,)),

time: 60.5 us -> 56 us (0.926)
  Pallas kernels: 56.9 us -> 52.5 us
    pallas_call x1, Pallas kernels: 56.9 us -> 52.5 us  [local(): pl.pallas_call(kernel, out_shape=(jax.ShapeDtypeStruct(q.shape, BF), jax....]
where the time goes in v4:
time: 56 us; the launch traced here: 55.5 us
  Pallas kernels  52.5 us (94%)
  local copies, waits for them, and re-layouts  2.29 us (4%)
  between operations  0.65 us (1%)
    pallas_call x1, Pallas kernels, local(): pl.pallas_call(kernel, out_shape=(jax.ShapeDtypeStruct(q.shape, BF), jax....  52.5 us
    unnamed x4, local copies, waits for them, and re-layouts  2.29 us

profile of v4, /device:TPU:1, one launch (start us, length us, event | category | flops | bytes accessed | tf_op | source)
XLA Modules:
  0.0 55.5 jit_solution(7749062662060562775)
XLA Ops:
  0.6 52.5 %shard_map.113 = (bf16[64,2048]{1,0:T(8,128)(2,1)}, bf16[4,2,2048]{2,1,0:T(2,128)(2,1)}) custom-call(bf16[64,2048]{1,0:T(8,128)(2,1)} %q_hbm.1, bf16[64,256]{1,0:T(8,128)(2,1)} %k_hbm.1, bf16[64,256]{1,0:T(8,128)(2,1)} %v_hbm.1, s32[128,128]{1,0:T(8,128)} %mask_hbm.1, s32[2]{0:T(128)} %widths_hbm.1, s32[2]{0:T(128)} %exps_hbm.1, bf16[4,2,2048]{2,1,0:T(2,128)(2,1)} %dq_hbm.1, ...), custom_call_target="tpu_custom_call" | custom-call | tf_op jit(solution)/shard_map/pallas_call | solution.py:498
  53.2 0.0 copy-start
  53.2 1.7 %copy.14 = bf16[64,2048]{1,0:T(8,128)(2,1)} copy(bf16[64,2048]{1,0:T(8,128)(2,1)} %get-tuple-element.4) | data formatting | bytes 524288
  54.8 0.0 copy-done
  54.8 0.6 %copy.15 = bf16[4,2,2048]{2,1,0:T(2,128)(2,1)} copy(bf16[4,2,2048]{2,1,0:T(2,128)(2,1)S(1)} %copy-done) | data formatting | bytes 65536
Async XLA Ops:
  53.2 1.7 %copy-start = (bf16[4,2,2048]{2,1,0:T(2,128)(2,1)S(1)}, bf16[4,2,2048]{2,1,0:T(2,128)(2,1)}, u32[]{:S(2)}) copy-start(bf16[4,2,2048]{2,1,0:T(2,128)(2,1)} %get-tuple-element.5) | copy-start | bytes 98308

commit v5 on v4

--- a/solution.py
+++ b/solution.py
@@ -33,28 +33,28 @@
     ((1, 0, 1), []),
     ((0, 1, 0), []),
     ((0, 1, 1), []),
+    ((1, 1, 0), []),
     ((2, 0, 0), [(0, 0)]),
-    ((2, 0, 1), []),
-    ((1, 1, 0), [(1, 0)]),
-    ((1, 1, 1), [(0, 1), (1, 1)]),
-    ((3, 0, 0), []),
-    ((3, 0, 1), [(0, 2)]),
+    ((1, 1, 1), []),
+    ((2, 0, 1), [(0, 1), (1, 0), (1, 1)]),
     ((2, 1, 0), []),
-    ((2, 1, 1), [(1, 2), (0, 3), (1, 3)]),
+    ((2, 1, 1), []),
+    ((3, 0, 0), [(0, 2)]),
+    ((3, 0, 1), [(0, 3), (1, 2)]),
+    ((3, 1, 0), [(1, 3)]),
+    ((3, 1, 1), [(0, 4)]),
     ((4, 0, 0), []),
-    ((4, 0, 1), []),
-    ((3, 1, 0), [(0, 4)]),
-    ((3, 1, 1), [(1, 4)]),
+    ((4, 0, 1), [(1, 4)]),
+    ((4, 1, 0), [(0, 5)]),
+    ((4, 1, 1), []),
+    ((5, 0, 0), [(1, 5), (0, 6), (1, 6)]),
+    ((5, 1, 0), []),
+    ((6, 0, 1), []),
     ((5, 0, 1), []),
-    ((5, 0, 0), [(0, 5), (1, 5)]),
-    ((4, 1, 0), []),
-    ((6, 0, 1), []),
-    ((4, 1, 1), []),
-    ((6, 0, 0), [(0, 6), (1, 6)]),
-    ((5, 1, 0), []),
-    ((5, 1, 1), []),
+    ((6, 0, 0), []),
+    ((6, 1, 1), []),
     ((6, 1, 0), []),
-    ((6, 1, 1), [(0, 7), (1, 7)]),
+    ((5, 1, 1), [(0, 7), (1, 7)]),
 ]
 ORDER = [g for g, _ in PLAN]
 NW = len(ORDER)
@@ -88,7 +88,8 @@
 OWN = START[-1]
 NTILE = OWN // TILE
 NEED = [max(k for k in range(NW) if START[k] < (t + 1) * TILE) for t in range(NTILE)]
-AFTER = {k: ORDER.index((d + 1, side, path)) for k, (d, side, path) in enumerate(ORDER) if d < 6}
+WAVE = {u: k for k in range(NW) for u in range(START[k], START[k + 1], HALF)}
+LAST = (2, 4)
 
 
 def hops(n, far, side):
@@ -107,12 +108,19 @@
     out = []
     for dx, dz in UNITS[k]:
         here = SLOT[(side, path, dx, dz)] * HALF
+        steps = []
         if path == 0 or dx == 0:
-            for way, n in hops(dz, 4, side):
-                out.append((path, "z", way, here, SLOT[(side, path, dx, n)] * HALF))
+            steps += [("z", way, (dx, n)) for way, n in hops(dz, 4, side)]
         if path == 1 or dz == 0:
-            for way, n in hops(dx, 2, side):
-                out.append((path, "x", way, here, SLOT[(side, path, n, dz)] * HALF))
+            steps += [("x", way, (n, dz)) for way, n in hops(dx, 2, side)]
+        steps = [m for m in steps if m[2] != LAST]
+        way = 1 if side == 0 else -1
+        if path == 0 and (dx, dz) == (2, -2 * way):
+            steps.append(("z", 2 * way, LAST))
+        if path == 1 and (dx, dz) == (0, 4):
+            steps.append(("x", 2 * way, LAST))
+        for axis, way, there in steps:
+            out.append((path, axis, way, here, SLOT[(side, path, *there)] * HALF))
     out.sort(key=lambda m: (m[0], m[1], m[2], m[3]))
     merged = []
     for path, axis, way, here, there in out:
@@ -203,12 +211,17 @@
         ("x", -1): at(yh, (x + XS - 1) % XS, z, core),
         ("z", 1): at(yh, x, (z + 1) % ZS, core),
         ("z", -1): at(yh, x, (z + ZS - 1) % ZS, core),
+        ("x", 2): at(yh, (x + 2) % XS, z, core),
+        ("z", 2): at(yh, x, (z + 2) % ZS, core),
+        ("z", -2): at(yh, x, (z + ZS - 2) % ZS, core),
     }
+    greeted = list(peers.values())
+    peers["x", -2] = peers["x", 2]
     across = at(1 - yh, x, z, core)
     sibling = at(yh, x, z, 1 - core)
 
     barrier = pltpu.get_barrier_semaphore()
-    for dev in (*peers.values(), across, sibling):
+    for dev in (*greeted, across, sibling):
         pl.semaphore_signal(barrier, inc=1, device_id=(dev, grp), device_id_type=MESH)
     pl.semaphore_signal(barrier, inc=1, device_id=(s, 1 - grp), device_id_type=MESH)
 
@@ -243,12 +256,11 @@
         )
 
     def forwards(k):
-        if k in AFTER:
-            n = AFTER[k]
-            for axis, way, here, there, count in messages(k):
-                remote(
-                    here, there, count, send_sem.at[n], recv_sem.at[n], peers[(axis, way)]
-                ).start()
+        for axis, way, here, there, count in messages(k):
+            n = WAVE[there]
+            remote(
+                here, there, count, send_sem.at[n], recv_sem.at[n], peers[(axis, way)]
+            ).start()
 
     def wave_copy(k):
         return remote(
@@ -272,7 +284,7 @@
     ]
     loads[0].wait()
     loads[1].wait()
-    pl.semaphore_wait(barrier, 7)
+    pl.semaphore_wait(barrier, len(greeted) + 3)
     for c in ycopies:
         c.start()
     for k in (0, 1):

time: 56 us -> 53 us (0.946)
  Pallas kernels: 52.5 us -> 49.9 us
    pallas_call x1, Pallas kernels: 52.5 us -> 49.9 us  [local(): pl.pallas_call(kernel, out_shape=(jax.ShapeDtypeStruct(q.shape, BF), jax....]
where the time goes in v5:
time: 53 us; the launch traced here: 52.9 us
  Pallas kernels  49.9 us (94%)
  local copies, waits for them, and re-layouts  2.29 us (4%)
  between operations  0.65 us (1%)
    pallas_call x1, Pallas kernels, local(): pl.pallas_call(kernel, out_shape=(jax.ShapeDtypeStruct(q.shape, BF), jax....  49.9 us
    unnamed x4, local copies, waits for them, and re-layouts  2.29 us

profile of v5, /device:TPU:1, one launch (start us, length us, event | category | flops | bytes accessed | tf_op | source)
XLA Modules:
  0.0 52.9 jit_solution(10270369578544360392)
XLA Ops:
  0.6 49.9 %shard_map.113 = (bf16[64,2048]{1,0:T(8,128)(2,1)}, bf16[4,2,2048]{2,1,0:T(2,128)(2,1)}) custom-call(bf16[64,2048]{1,0:T(8,128)(2,1)} %q_hbm.1, bf16[64,256]{1,0:T(8,128)(2,1)} %k_hbm.1, bf16[64,256]{1,0:T(8,128)(2,1)} %v_hbm.1, s32[128,128]{1,0:T(8,128)} %mask_hbm.1, s32[2]{0:T(128)} %widths_hbm.1, s32[2]{0:T(128)} %exps_hbm.1, bf16[4,2,2048]{2,1,0:T(2,128)(2,1)} %dq_hbm.1, ...), custom_call_target="tpu_custom_call" | custom-call | tf_op jit(solution)/shard_map/pallas_call | solution.py:510
  50.6 0.0 copy-start
  50.6 1.7 %copy.14 = bf16[64,2048]{1,0:T(8,128)(2,1)} copy(bf16[64,2048]{1,0:T(8,128)(2,1)} %get-tuple-element.4) | data formatting | bytes 524288
  52.3 0.0 copy-done
  52.3 0.6 %copy.15 = bf16[4,2,2048]{2,1,0:T(2,128)(2,1)} copy(bf16[4,2,2048]{2,1,0:T(2,128)(2,1)S(1)} %copy-done) | data formatting | bytes 65536
Async XLA Ops:
  50.6 1.7 %copy-start = (bf16[4,2,2048]{2,1,0:T(2,128)(2,1)S(1)}, bf16[4,2,2048]{2,1,0:T(2,128)(2,1)}, u32[]{:S(2)}) copy-start(bf16[4,2,2048]{2,1,0:T(2,128)(2,1)} %get-tuple-element.5) | copy-start | bytes 98308

commit v6 on v5

--- a/solution.py
+++ b/solution.py
@@ -50,11 +50,11 @@
     ((5, 0, 0), [(1, 5), (0, 6), (1, 6)]),
     ((5, 1, 0), []),
     ((6, 0, 1), []),
-    ((5, 0, 1), []),
+    ((5, 0, 1), [(0, 7)]),
     ((6, 0, 0), []),
     ((6, 1, 1), []),
     ((6, 1, 0), []),
-    ((5, 1, 1), [(0, 7), (1, 7)]),
+    ((5, 1, 1), [(1, 7), (0, 8), (1, 8)]),
 ]
 ORDER = [g for g, _ in PLAN]
 NW = len(ORDER)
@@ -86,8 +86,8 @@
 START.append(len(SLOT) * HALF)
 SOURCES = list(SLOT)
 OWN = START[-1]
-NTILE = OWN // TILE
-NEED = [max(k for k in range(NW) if START[k] < (t + 1) * TILE) for t in range(NTILE)]
+TILES = [(i * TILE, TILE) for i in range(OWN // TILE - 1)] + [(OWN - 512, 256), (OWN - 256, 256)]
+NEED = [max(k for k in range(NW) if START[k] < t + n) for t, n in TILES]
 WAVE = {u: k for k in range(NW) for u in range(START[k], START[k + 1], HALF)}
 LAST = (2, 4)
 
@@ -388,23 +388,24 @@
     part_core = [(core + o) % 2 for o in (0, 1)]
 
     def compute(e, tile):
-        first = e * OWN + tile * TILE
-        for u in range(TILE // HALF):
-            side, path, dx, dz = SOURCES[tile * (TILE // HALF) + u]
+        base, rows = TILES[tile]
+        first = e * OWN + base
+        for u in range(rows // HALF):
+            side, path, dx, dz = SOURCES[base // HALF + u]
             block = part_y[side] + part_x[dx % XS] + part_z[dz % ZS] + part_core[e]
             here = slice(u * HALF, (u + 1) * HALF)
             oh[here, :] = jnp.where(lanes_in == block, 1.0, 0.0).astype(BF)
             pos[here, :] = rows_in + (block * TOK + path * HALF)
 
-        keys = kv[pl.ds(first, TILE), 0:256]
-        blocks = oh[...]
+        keys = kv[pl.ds(first, rows), 0:256]
+        blocks = oh[0:rows, :]
         scores = [
             dot(
                 jnp.concatenate([keys[:, kh * HEAD : (kh + 1) * HEAD], blocks], axis=1), qx[kh]
             )
             for kh in range(KV)
         ]
-        vals_t = kv[pl.ds(first, TILE), 256:512].T
+        vals_t = kv[pl.ds(first, rows), 256:512].T
 
         def code(rot, axis):
             return jnp.concatenate(
@@ -431,7 +432,7 @@
             m_p[kh] = top
             l_p[kh] = l_p[kh] * fade + jnp.sum(w, axis=0, keepdims=True)
             o_p[kh] = o_p[kh] * fade + dot(vals_t[kh * HEAD : (kh + 1) * HEAD, :], w.astype(BF))
-        sc = jnp.where(pos[...] < limits, two[:, 0:128] + two[:, 128:256], VERY_LOW)
+        sc = jnp.where(pos[0:rows, :] < limits, two[:, 0:128] + two[:, 128:256], VERY_LOW)
         old = m_d[...]
         top = jnp.maximum(old, jnp.max(sc, axis=0, keepdims=True))
         w = jnp.exp2(sc * SCORE - top * SCORE)

time: 53 us -> 53.9 us (1.017)
  Pallas kernels: 49.9 us -> 50.9 us
    pallas_call x1, Pallas kernels: 49.9 us -> 50.9 us  [local(): pl.pallas_call(kernel, out_shape=(jax.ShapeDtypeStruct(q.shape, BF), jax....]
where the time goes in v6:
time: 53.9 us; the launch traced here: 53.8 us
  Pallas kernels  50.9 us (94%)
  local copies, waits for them, and re-layouts  2.29 us (4%)
  between operations  0.65 us (1%)
    pallas_call x1, Pallas kernels, local(): pl.pallas_call(kernel, out_shape=(jax.ShapeDtypeStruct(q.shape, BF), jax....  50.9 us
    unnamed x4, local copies, waits for them, and re-layouts  2.29 us

profile of v6, /device:TPU:1, one launch (start us, length us, event | category | flops | bytes accessed | tf_op | source)
XLA Modules:
  0.0 53.8 jit_solution(14570727472945720601)
XLA Ops:
  0.6 50.9 %shard_map.113 = (bf16[64,2048]{1,0:T(8,128)(2,1)}, bf16[4,2,2048]{2,1,0:T(2,128)(2,1)}) custom-call(bf16[64,2048]{1,0:T(8,128)(2,1)} %q_hbm.1, bf16[64,256]{1,0:T(8,128)(2,1)} %k_hbm.1, bf16[64,256]{1,0:T(8,128)(2,1)} %v_hbm.1, s32[128,128]{1,0:T(8,128)} %mask_hbm.1, s32[2]{0:T(128)} %widths_hbm.1, s32[2]{0:T(128)} %exps_hbm.1, bf16[4,2,2048]{2,1,0:T(2,128)(2,1)} %dq_hbm.1, ...), custom_call_target="tpu_custom_call" | custom-call | tf_op jit(solution)/shard_map/pallas_call | solution.py:511
  51.5 0.0 copy-start
  51.5 1.7 %copy.14 = bf16[64,2048]{1,0:T(8,128)(2,1)} copy(bf16[64,2048]{1,0:T(8,128)(2,1)} %get-tuple-element.4) | data formatting | bytes 524288
  53.2 0.0 copy-done
  53.2 0.6 %copy.15 = bf16[4,2,2048]{2,1,0:T(2,128)(2,1)} copy(bf16[4,2,2048]{2,1,0:T(2,128)(2,1)S(1)} %copy-done) | data formatting | bytes 65536
Async XLA Ops:
  51.5 1.7 %copy-start = (bf16[4,2,2048]{2,1,0:T(2,128)(2,1)S(1)}, bf16[4,2,2048]{2,1,0:T(2,128)(2,1)}, u32[]{:S(2)}) copy-start(bf16[4,2,2048]{2,1,0:T(2,128)(2,1)} %get-tuple-element.5) | copy-start | bytes 98308
